TPU v7x, 256 devices: a 4x2x16 block of a 4x16x16 slice. The times are simulated.
256 devices in a mesh: grp: 2 (over y), row: 128 (over z, x, core).
Axes of the slice: x: 4, y: 2, z: 16, core: 2. Of those that a mesh axis runs over, the one named last changes fastest.
The devices are a block of a 4x16x16 slice.
Arguments:
- cells: float32 [2048, 128, 192], P(('grp', 'row')), parts along dimension 0, may hold values from -6 to 6
- n_train: int32 [2], P('grp'), parts along dimension 0, may hold values from 128 to 1023
- present: int32 [256], P('grp'), parts along dimension 0, may hold values from 0 to 1, as said below
- norm_gain: float32 [3, 192], replicated, may hold values from 0.1 to 1.9
- feat_qkv: bfloat16 [3, 192, 192], replicated, may hold values from -6 to 6
- feat_out: bfloat16 [192, 192], replicated, may hold values from -0.4375 to 0.4375
- item_qkv: bfloat16 [3, 192, 192], replicated, may hold values from -6 to 6
- item_out: bfloat16 [192, 192], replicated, may hold values from -0.875 to 0.875
- mlp_in: bfloat16 [192, 768], replicated, may hold values from -0.4375 to 0.4375
- mlp_out: bfloat16 [768, 192], replicated, may hold values from -0.21875 to 0.21875
Outputs:
- result: float32 [2048, 128, 192], P(('grp', 'row')), parts along dimension 0
There are 2 independent parts, one for each index of `grp`. A program takes and returns all parts, laid end to end along the dimension named above; an argument that names none is the same for every part. Nothing has to cross between parts.
Inputs may be any that keep to these rules, and one draw needn't show every extreme that they name: At least one of the 128 features is present.
All inputs are finite; a program needn't handle non-finite values.
Results may differ from a plain program's by a relative error of at most 0.03.
The roundings to bfloat16 on the way count: a program that leaves them out, or rounds other values in their place, can miss the bound.
Values may be sent and summed in bfloat16 or wider, within the bound.
No kernel may reach another device: no remote copies, remote signals or barrier semaphores. Data moves between devices by JAX's collectives and lax.ppermute only.
A program may use at most 64 MiB of HBM per device.

v0:
```python
import math

import jax
import jax.numpy as jnp
from jax import lax
from jax.experimental import pallas as pl
from jax.experimental.pallas import tpu as pltpu
from jax.sharding import PartitionSpec as P

HEADS = 6
ROW = "row"
GRP_ROW = ("grp", "row")
f32 = jnp.float32
bf16 = jnp.bfloat16

norm_floor = 0.25
masked_score = -1e30


def nn(a, b):
    return lax.dot_general(a, b, (((1,), (0,)), ((), ())), preferred_element_type=f32)


def nt(a, b):
    return lax.dot_general(a, b, (((1,), (1,)), ((), ())), preferred_element_type=f32)


def tn(a, b):
    return lax.dot_general(a, b, (((0,), (0,)), ((), ())), preferred_element_type=f32)


def iota(shape, dim):
    return lax.broadcasted_iota(jnp.int32, shape, dim)


def onehot(mask):
    return jnp.where(mask, 1.0, 0.0).astype(bf16)


def layer_norm(v, gain):
    width = v.shape[-1]
    mean = jnp.sum(v, axis=-1, keepdims=True) * (1.0 / width)
    c = v - mean
    var = jnp.sum(c * c, axis=-1, keepdims=True) * (1.0 / width)
    return c * lax.rsqrt(var + norm_floor) * gain


def flipped(w):
    n = w.shape[0]
    eye = onehot(iota((n, n), 0) == iota((n, n), 1))
    return nt(eye, w).astype(bf16)


def spread_keys(w, head):
    n = w.shape[0]
    shape = (n, HEADS * 128)
    col = iota(shape, 1)
    lane = col & 127
    place = onehot((iota(shape, 0) == (col >> 7) * head + (lane & (head - 1))) & (lane < 3 * head))
    return nn(w, place).astype(bf16)


def prepare_weights(qkv, wq, wk, wv, head):
    wq[...] = flipped(qkv[0])
    wk[...] = spread_keys(qkv[1], head)
    wv[...] = flipped(qkv[2])


def fill_constant_rows(qs, vs, head):
    for h in range(HEADS):
        cols = qs.shape[-1]
        one_row = onehot(iota((head, cols), 0) == 0)
        qs[h, 3 * head : 4 * head, :] = one_row
        vs[h, head : head + 16, :] = jnp.ones((16, cols), bf16)


def project(x, bias, rows, wq, wk, wv, qs, ks, vs, head):
    scale = (1.0 / math.sqrt(head)) * math.log2(math.e)
    q = nt(wq[...], x) * scale
    qh = q.astype(bf16)
    ql = (q - qh.astype(f32)).astype(bf16)
    v = nt(wv[...], x).astype(bf16)
    for h in range(HEADS):
        mine = slice(h * head, (h + 1) * head)
        qs[h, 0:head, rows] = qh[mine]
        qs[h, head : 2 * head, rows] = ql[mine]
        qs[h, 2 * head : 3 * head, rows] = qh[mine]
        vs[h, 0:head, rows] = v[mine]
    lane = iota((x.shape[0], 128), 1)
    for h in range(HEADS):
        k = nn(x, wk[:, h * 128 : (h + 1) * 128])
        kh = k.astype(bf16).astype(f32)
        kl = k - kh
        packed = jnp.where(lane < 2 * head, kh, jnp.where(lane < 3 * head, kl, bias))
        ks[rows, h * 128 : (h + 1) * 128] = packed.astype(bf16)


def pack_maps(tokens, inner_rows, peers):
    rows = peers * (inner_rows + inner_rows // 2)
    shape = (rows, tokens)
    return iota(shape, 0), iota(shape, 1)


def front_kernel(present, cells, gain, qkv, wout, mid, send, xn, qs, ks, vs, ctx, wq, wk, wv):
    tokens, width = cells.shape
    head = width // HEADS
    feats = present.shape[-1]
    rows = tokens // feats
    prepare_weights(qkv, wq, wk, wv, head)
    fill_constant_rows(qs, vs, head)
    g0 = gain[0:1, :]
    for r in range(rows):
        at = slice(r * feats, (r + 1) * feats)
        xn[at, :] = layer_norm(cells[at, :], g0).astype(bf16)
    eye = iota((feats, feats), 0) == iota((feats, feats), 1)
    absent = jnp.where(present[...] > 0, 0.0, masked_score)
    bias = jnp.sum(jnp.where(eye, absent, 0.0), axis=1, keepdims=True)
    bias = jnp.concatenate([bias, bias], axis=0)
    step = 2 * feats
    for c in range(tokens // step):
        at = slice(c * step, (c + 1) * step)
        project(xn[at, :], bias, at, wq, wk, wv, qs, ks, vs, head)
    for r in range(rows):
        at = slice(r * feats, (r + 1) * feats)
        scores = [nn(ks[at, h * 128 : (h + 1) * 128], qs[h, :, at]) for h in range(HEADS)]
        weights = []
        for s in scores:
            top = jnp.max(s, axis=0, keepdims=True)
            weights.append(jnp.exp2(s - top).astype(bf16))
        for h in range(HEADS):
            o = nn(vs[h, :, at], weights[h])
            ctx[h * head : (h + 1) * head, at] = (o[0:head] * (1.0 / o[head : head + 1])).astype(bf16)
    g1 = gain[1:2, :]
    for r in range(rows):
        at = slice(r * feats, (r + 1) * feats)
        m = cells[at, :] + tn(ctx[:, at], wout[...])
        mid[at, :] = m
        xn[at, :] = layer_norm(m, g1).astype(bf16)
    o, t = pack_maps(rows * 16, rows, 16)
    f, r = t & 15, t >> 4
    base = f * 12
    low = onehot(o == base + r)
    first = onehot((o == base + 8 + (r & 3)) & (r < 4))
    second = onehot((o == base + 8 + (r & 3)) & (r >= 4))
    out_rows = o.shape[0]
    lane = iota((out_rows, 128), 1)
    for b in range(feats // 16):
        x = jnp.concatenate([xn[k * feats + b * 16 : k * feats + b * 16 + 16, :] for k in range(rows)], axis=0)
        tail = x[:, 128:width]
        tails = jnp.concatenate([tail, tail], axis=1)
        out = nn(low, x[:, 0:128]) + jnp.where(lane < 64, nn(first, tails), nn(second, tails))
        send[b * out_rows : (b + 1) * out_rows, :] = out.astype(bf16)


def rows_kernel(n_train, got, qkv, send, xn, qs, ks, vs, ctx, wq, wk, wv):
    width = qkv.shape[-1]
    head = width // HEADS
    total = xn.shape[0]
    prepare_weights(qkv, wq, wk, wv, head)
    fill_constant_rows(qs, vs, head)
    t, p = iota((128, 192), 0), iota((128, 192), 1)
    low = onehot(p == (t >> 3) * 12 + (t & 7))
    high = onehot(p == (t >> 3) * 12 + 8 + (t & 3))
    early = (iota((128, 64), 0) & 7) < 4
    for b in range(total // 128):
        a = got[b * 192 : (b + 1) * 192, :]
        hi = nn(high, a)
        xn[b * 128 : (b + 1) * 128, 0:128] = nn(low, a).astype(bf16)
        xn[b * 128 : (b + 1) * 128, 128:width] = jnp.where(early, hi[:, 0:64], hi[:, 64:128]).astype(bf16)
    live = n_train[0]
    step = 256
    for c in range(total // step):
        at = slice(c * step, (c + 1) * step)
        bias = jnp.where(iota((step, 1), 0) + c * step < live, 0.0, masked_score)
        project(xn[at, :], bias, at, wq, wk, wv, qs, ks, vs, head)

    def query_tile(j, carry):
        cols = pl.ds(pl.multiple_of(j * 256, 256), 256)

        def score(h):
            return nn(ks[:, h * 128 : (h + 1) * 128], qs[h, :, cols])

        s = score(0)
        for h in range(HEADS):
            ahead = score(h + 1) if h + 1 < HEADS else None
            top = jnp.max(s, axis=0, keepdims=True)
            w = jnp.exp2(s - top).astype(bf16)
            o = nn(vs[h], w)
            ctx[h * head : (h + 1) * head, cols] = (o[0:head] * (1.0 / o[head : head + 1])).astype(bf16)
            s = ahead
        return carry

    lax.fori_loop(0, total // 256, query_tile, 0)
    o, q = iota((192, 128), 0), iota((192, 128), 1)
    base, r = (q >> 3) * 12, q & 7
    low = onehot(o == base + r)
    first = onehot((o == base + 8 + (r & 3)) & (r < 4))
    second = onehot((o == base + 8 + (r & 3)) & (r >= 4))
    lane = iota((192, 128), 1)
    for b in range(total // 128):
        at = slice(b * 128, (b + 1) * 128)
        tail = ctx[128:width, at]
        tails = jnp.concatenate([tail, tail], axis=0)
        out = nt(low, ctx[0:128, at]) + jnp.where(lane < 64, nt(first, tails), nt(second, tails))
        send[b * 192 : (b + 1) * 192, :] = out.astype(bf16)


def tail_kernel(got, mid, gain, wout, w_in, w_out, result, ctx):
    tokens, width = mid.shape
    feats = tokens // 8
    t, p = iota((128, 192), 0), iota((128, 192), 1)
    low = onehot(p == (t & 15) * 12 + (t >> 4))
    high = onehot(p == (t & 15) * 12 + 8 + ((t >> 4) & 3))
    early = iota((128, 64), 0) < 64
    for b in range(feats // 16):
        a = got[b * 192 : (b + 1) * 192, :]
        hi = nn(high, a)
        lo = nn(low, a).astype(bf16)
        hi = jnp.where(early, hi[:, 0:64], hi[:, 64:128]).astype(bf16)
        for r in range(8):
            at = slice(r * feats + b * 16, r * feats + b * 16 + 16)
            ctx[at, 0:128] = lo[r * 16 : (r + 1) * 16]
            ctx[at, 128:width] = hi[r * 16 : (r + 1) * 16]
    g2 = gain[2:3, :]
    step = 256
    for c in range(tokens // step):
        at = slice(c * step, (c + 1) * step)
        late = mid[at, :] + nn(ctx[at, :], wout[...])
        n3 = layer_norm(late, g2).astype(bf16)
        z = nn(n3, w_in[...])
        hidden = (z * 0.5 * (1.0 + lax.erf(z * math.sqrt(0.5)))).astype(bf16)
        result[at, :] = late + nn(hidden, w_out[...])


def scratch(tokens, width):
    head = width // HEADS
    return [
        pltpu.VMEM((tokens, width), bf16),
        pltpu.VMEM((HEADS, 4 * head, tokens), bf16),
        pltpu.VMEM((tokens, HEADS * 128), bf16),
        pltpu.VMEM((HEADS, head + 16, tokens), bf16),
        pltpu.VMEM((width, tokens), bf16),
        pltpu.VMEM((width, width), bf16),
        pltpu.VMEM((width, HEADS * 128), bf16),
        pltpu.VMEM((width, width), bf16),
    ]


VMEM = pl.BlockSpec(memory_space=pltpu.VMEM)
SMEM = pl.BlockSpec(memory_space=pltpu.SMEM)


def front(present, cells, gain, qkv, wout):
    tokens, width = cells.shape
    return pl.pallas_call(
        front_kernel,
        out_shape=(
            jax.ShapeDtypeStruct((tokens, width), f32),
            jax.ShapeDtypeStruct((tokens * width // 128, 128), bf16),
        ),
        in_specs=[VMEM] * 5,
        out_specs=(VMEM, VMEM),
        scratch_shapes=scratch(tokens, width),
        name="front",
    )(present, cells, gain, qkv, wout)


def rows(n_train, got, qkv):
    width = qkv.shape[-1]
    tokens = got.shape[0] * 128 // width
    return pl.pallas_call(
        rows_kernel,
        out_shape=jax.ShapeDtypeStruct(got.shape, bf16),
        in_specs=[SMEM, VMEM, VMEM],
        out_specs=VMEM,
        scratch_shapes=scratch(tokens, width),
        name="rows",
    )(n_train, got, qkv)


def tail(got, mid, gain, wout, w_in, w_out):
    return pl.pallas_call(
        tail_kernel,
        out_shape=jax.ShapeDtypeStruct(mid.shape, f32),
        in_specs=[VMEM] * 6,
        out_specs=VMEM,
        scratch_shapes=[pltpu.VMEM(mid.shape, bf16)],
        name="tail",
    )(got, mid, gain, wout, w_in, w_out)


def exchanged(block):
    peers = lax.axis_size(ROW)
    tiles = block.reshape(peers, 3, 4, 128)
    return lax.all_to_all(tiles, ROW, 0, 0, tiled=True).reshape(block.shape)


def body(
    cells, n_train, present, norm_gain, feat_qkv, feat_out, item_qkv, item_out, mlp_in, mlp_out
):
    row_dev, feature_count, width = cells.shape
    flat = cells.reshape(row_dev * feature_count, width)
    mid, send = front(present.reshape(1, feature_count), flat, norm_gain, feat_qkv, feat_out)
    got = exchanged(send)
    back = rows(n_train, got, item_qkv)
    returned = exchanged(back)
    out = tail(returned, mid, norm_gain, item_out, mlp_in, mlp_out)
    return out.reshape(cells.shape)


def solution(mesh):
    return jax.shard_map(
        body,
        mesh=mesh,
        in_specs=(P(GRP_ROW, None, None), P("grp"), P("grp"), P(), P(), P(), P(), P(), P(), P()),
        out_specs=P(GRP_ROW, None, None),
        check_vma=False,
    )
```

profile of v0, /device:TPU:33, one launch (start us, length us, event | category | flops | bytes accessed | tf_op | source)
XLA Modules:
  0.0 124.3 jit_solution(11791887970762448713)
XLA Ops:
  0.0 2.5 %copy.11 = f32[8,128,192]{2,1,0:T(8,128)} copy(f32[8,128,192]{1,2,0:T(8,128)} %param.10) | data formatting | bytes 1572864 | tf_op args[0]
  2.5 7.0 %front.1 = (f32[1024,192]{1,0:T(8,128)}, bf16[1536,128]{1,0:T(8,128)(2,1)}) custom-call(s32[1,128]{1,0:T(1,128)} %bitcast.13, f32[1024,192]{1,0:T(8,128)} %bitcast.8, f32[3,192]{1,0:T(4,128)} %gain.3, bf16[3,192,192]{2,1,0:T(8,128)(2,1)} %qkv.2, bf16[192,192]{1,0:T(8,128)(2,1)} %wout.2), custom_call_target="tpu_custom_call" | custom-call | tf_op jit(solution)/shard_map/front/pallas_call | solution.py:255
  9.5 31.0 %all-to-all-start = ((bf16[128,3,4,128]{3,2,1,0:T(4,128)(2,1)}), bf16[128,3,4,128]{3,2,1,0:T(4,128)(2,1)S(1)}, u32[]{:S(2)}, u32[]{:S(2)}) async-start(bf16[128,3,4,128]{3,2,1,0:T(4,128)(2,1)} %bitcast.12), calls=%async_computation | async-start | bytes 786432 | tf_op jit(solution)/shard_map/all_to_all | solution.py:295
  41.2 24.5 %all-to-all-done = bf16[128,3,4,128]{3,2,1,0:T(4,128)(2,1)S(1)} async-done(((bf16[128,3,4,128]{3,2,1,0:T(4,128)(2,1)}), bf16[128,3,4,128]{3,2,1,0:T(4,128)(2,1)S(1)}, u32[]{:S(2)}, u32[]{:S(2)}) %all-to-all-start) | async-done | bytes 393248 | tf_op jit(solution)/shard_map/all_to_all | solution.py:295
  65.7 0.0 copy-start.1
  65.7 0.7 copy-done.1
  66.5 14.3 %rows.1 = bf16[1536,128]{1,0:T(8,128)(2,1)} custom-call(s32[1]{0:T(128)S(6)} %copy.14.n_train, bf16[1536,128]{1,0:T(8,128)(2,1)} %bitcast.10, bf16[3,192,192]{2,1,0:T(8,128)(2,1)} %qkv.3), custom_call_target="tpu_custom_call" | custom-call | tf_op jit(solution)/shard_map/rows/pallas_call | solution.py:271
  80.7 0.0 copy-start.2
  80.7 10.2 %all-to-all-start.1 = ((bf16[128,3,4,128]{3,2,1,0:T(4,128)(2,1)}), bf16[128,3,4,128]{3,2,1,0:T(4,128)(2,1)S(1)}, u32[]{:S(2)}, u32[]{:S(2)}) async-start(bf16[128,3,4,128]{3,2,1,0:T(4,128)(2,1)} %bitcast.11), calls=%async_computation.1 | async-start | bytes 786432 | tf_op jit(solution)/shard_map/all_to_all | solution.py:295
  90.9 0.0 copy-done.2
  90.9 0.9 copy.12.w_out
  91.9 24.2 %all-to-all-done.1 = bf16[128,3,4,128]{3,2,1,0:T(4,128)(2,1)S(1)} async-done(((bf16[128,3,4,128]{3,2,1,0:T(4,128)(2,1)}), bf16[128,3,4,128]{3,2,1,0:T(4,128)(2,1)S(1)}, u32[]{:S(2)}, u32[]{:S(2)}) %all-to-all-start.1) | async-done | bytes 393248 | tf_op jit(solution)/shard_map/all_to_all | solution.py:295
  116.1 0.0 copy-start
  116.1 0.7 copy-done
  116.8 5.0 %tail.1 = f32[1024,192]{1,0:T(8,128)} custom-call(bf16[1536,128]{1,0:T(8,128)(2,1)} %bitcast.9, f32[1024,192]{1,0:T(8,128)} %get-tuple-element.8.mid, f32[3,192]{1,0:T(4,128)} %gain.3, bf16[192,192]{1,0:T(8,128)(2,1)} %wout.3, bf16[192,768]{1,0:T(8,128)(2,1)} %w_in.1, bf16[768,192]{1,0:T(8,128)(2,1)} %copy.12.w_out), custom_call_target="tpu_custom_call" | custom-call | tf_op jit(solution)/shard_map/tail/pallas_call | solution.py:282
  121.9 2.4 %copy.13 = f32[8,128,192]{1,2,0:T(8,128)} copy(f32[8,128,192]{2,1,0:T(8,128)} %bitcast.7) | data formatting | bytes 1572864 | tf_op jit(solution)/shard_map/reshape | solution.py:308
Async XLA Ops:
  9.5 56.2 %all-to-all-start = ((bf16[128,3,4,128]{3,2,1,0:T(4,128)(2,1)}), bf16[128,3,4,128]{3,2,1,0:T(4,128)(2,1)S(1)}, u32[]{:S(2)}, u32[]{:S(2)}) async-start(bf16[128,3,4,128]{3,2,1,0:T(4,128)(2,1)} %bitcast.12), calls=%async_computation | async-start | bytes 786432 | tf_op jit(solution)/shard_map/all_to_all | solution.py:295
  65.7 0.7 copy-start.1
  80.7 10.2 %copy-start.2 = (bf16[768,192]{0,1:T(8,128)(2,1)S(1)}, bf16[768,192]{0,1:T(8,128)(2,1)}, u32[]{:S(2)}) copy-start(bf16[768,192]{0,1:T(8,128)(2,1)} %param.19) | copy-start | bytes 884740
  80.7 35.4 %all-to-all-start.1 = ((bf16[128,3,4,128]{3,2,1,0:T(4,128)(2,1)}), bf16[128,3,4,128]{3,2,1,0:T(4,128)(2,1)S(1)}, u32[]{:S(2)}, u32[]{:S(2)}) async-start(bf16[128,3,4,128]{3,2,1,0:T(4,128)(2,1)} %bitcast.11), calls=%async_computation.1 | async-start | bytes 786432 | tf_op jit(solution)/shard_map/all_to_all | solution.py:295
  116.1 0.7 copy-start
where the time goes:
time: 125 us; the launch traced here: 124 us
  waiting for transfers between devices  48.7 us (39%)
  starting transfers between devices  41.2 us (33%)
  Pallas kernels  26.3 us (21%)
  local copies, waits for them, and re-layouts  7.35 us (6%)
    all_to_all x2, waiting for transfers between devices, exchanged(): return lax.all_to_all(tiles, ROW, 0, 0, tiled=True).reshape(block.shape)  48.7 us
    all_to_all x2, starting transfers between devices, exchanged(): return lax.all_to_all(tiles, ROW, 0, 0, tiled=True).reshape(block.shape)  41.2 us
    pallas_call x1, Pallas kernels, rows(): pl.pallas_call(rows_kernel, out_shape=jax.ShapeDtypeStruct(got.shape, bf1...  14.3 us
    pallas_call x1, Pallas kernels, front(): pl.pallas_call(front_kernel, out_shape=(jax.ShapeDtypeStruct((tokens, wid...  7.03 us
    pallas_call x1, Pallas kernels, tail(): pl.pallas_call(tail_kernel, out_shape=jax.ShapeDtypeStruct(mid.shape, f32...  5.04 us
    unnamed x8, local copies, waits for them, and re-layouts  4.91 us
  transfers between devices with their start and end apart: 2, of which 2 were waited for; matrix products, arithmetic and copies ran while one was open for 1% of the time, Pallas kernels for 0%

commit v1 on v0

--- a/solution.py
+++ b/solution.py
@@ -38,11 +38,17 @@
 
 
 def layer_norm(v, gain):
-    width = v.shape[-1]
-    mean = jnp.sum(v, axis=-1, keepdims=True) * (1.0 / width)
+    scale = 1.0 / v.shape[0]
+    mean = jnp.sum(v, axis=0, keepdims=True) * scale
     c = v - mean
-    var = jnp.sum(c * c, axis=-1, keepdims=True) * (1.0 / width)
+    var = jnp.sum(c * c, axis=0, keepdims=True) * scale
     return c * lax.rsqrt(var + norm_floor) * gain
+
+
+def column(row):
+    n = row.shape[-1]
+    eye = iota((n, n), 0) == iota((n, n), 1)
+    return jnp.sum(jnp.where(eye, row, 0.0), axis=1, keepdims=True)
 
 
 def flipped(w):
@@ -74,12 +80,12 @@
         vs[h, head : head + 16, :] = jnp.ones((16, cols), bf16)
 
 
-def project(x, bias, rows, wq, wk, wv, qs, ks, vs, head):
+def project(xt, x, bias, rows, wq, wk, wv, qs, ks, vs, head):
     scale = (1.0 / math.sqrt(head)) * math.log2(math.e)
-    q = nt(wq[...], x) * scale
+    q = (nn(wq[...], xt) if xt is not None else nt(wq[...], x)) * scale
     qh = q.astype(bf16)
     ql = (q - qh.astype(f32)).astype(bf16)
-    v = nt(wv[...], x).astype(bf16)
+    v = (nn(wv[...], xt) if xt is not None else nt(wv[...], x)).astype(bf16)
     for h in range(HEADS):
         mine = slice(h * head, (h + 1) * head)
         qs[h, 0:head, rows] = qh[mine]
@@ -95,31 +101,19 @@
         ks[rows, h * 128 : (h + 1) * 128] = packed.astype(bf16)
 
 
-def pack_maps(tokens, inner_rows, peers):
-    rows = peers * (inner_rows + inner_rows // 2)
-    shape = (rows, tokens)
-    return iota(shape, 0), iota(shape, 1)
-
-
 def front_kernel(present, cells, gain, qkv, wout, mid, send, xn, qs, ks, vs, ctx, wq, wk, wv):
-    tokens, width = cells.shape
+    rows, width, feats = cells.shape
     head = width // HEADS
-    feats = present.shape[-1]
-    rows = tokens // feats
     prepare_weights(qkv, wq, wk, wv, head)
+    wo = flipped(wout[...])
     fill_constant_rows(qs, vs, head)
-    g0 = gain[0:1, :]
-    for r in range(rows):
-        at = slice(r * feats, (r + 1) * feats)
-        xn[at, :] = layer_norm(cells[at, :], g0).astype(bf16)
-    eye = iota((feats, feats), 0) == iota((feats, feats), 1)
-    absent = jnp.where(present[...] > 0, 0.0, masked_score)
-    bias = jnp.sum(jnp.where(eye, absent, 0.0), axis=1, keepdims=True)
+    g0 = jnp.broadcast_to(column(gain[0:1, :]), (width, feats))
+    g1 = jnp.broadcast_to(column(gain[1:2, :]), (width, feats))
+    bias = column(jnp.where(present[...] > 0, 0.0, masked_score))
     bias = jnp.concatenate([bias, bias], axis=0)
-    step = 2 * feats
-    for c in range(tokens // step):
-        at = slice(c * step, (c + 1) * step)
-        project(xn[at, :], bias, at, wq, wk, wv, qs, ks, vs, head)
+    for c in range(rows // 2):
+        xt = jnp.concatenate([layer_norm(cells[2 * c + k], g0).astype(bf16) for k in range(2)], axis=1)
+        project(xt, xt.T, bias, slice(c * 2 * feats, (c + 1) * 2 * feats), wq, wk, wv, qs, ks, vs, head)
     for r in range(rows):
         at = slice(r * feats, (r + 1) * feats)
         scores = [nn(ks[at, h * 128 : (h + 1) * 128], qs[h, :, at]) for h in range(HEADS)]
@@ -130,26 +124,27 @@
         for h in range(HEADS):
             o = nn(vs[h, :, at], weights[h])
             ctx[h * head : (h + 1) * head, at] = (o[0:head] * (1.0 / o[head : head + 1])).astype(bf16)
-    g1 = gain[1:2, :]
-    for r in range(rows):
-        at = slice(r * feats, (r + 1) * feats)
-        m = cells[at, :] + tn(ctx[:, at], wout[...])
-        mid[at, :] = m
-        xn[at, :] = layer_norm(m, g1).astype(bf16)
-    o, t = pack_maps(rows * 16, rows, 16)
+    for c in range(rows // 2):
+        both = nn(wo, ctx[:, c * 2 * feats : (c + 1) * 2 * feats])
+        for k in range(2):
+            r = 2 * c + k
+            m = cells[r] + both[:, k * feats : (k + 1) * feats]
+            mid[r] = m
+            xn[r * feats : (r + 1) * feats, :] = layer_norm(m, g1).astype(bf16).T
+    shape = (192, rows * 16)
+    o, t = iota(shape, 0), iota(shape, 1)
     f, r = t & 15, t >> 4
     base = f * 12
     low = onehot(o == base + r)
     first = onehot((o == base + 8 + (r & 3)) & (r < 4))
     second = onehot((o == base + 8 + (r & 3)) & (r >= 4))
-    out_rows = o.shape[0]
-    lane = iota((out_rows, 128), 1)
+    lane = iota((192, 128), 1)
     for b in range(feats // 16):
         x = jnp.concatenate([xn[k * feats + b * 16 : k * feats + b * 16 + 16, :] for k in range(rows)], axis=0)
         tail = x[:, 128:width]
         tails = jnp.concatenate([tail, tail], axis=1)
         out = nn(low, x[:, 0:128]) + jnp.where(lane < 64, nn(first, tails), nn(second, tails))
-        send[b * out_rows : (b + 1) * out_rows, :] = out.astype(bf16)
+        send[b * 192 : (b + 1) * 192, :] = out.astype(bf16)
 
 
 def rows_kernel(n_train, got, qkv, send, xn, qs, ks, vs, ctx, wq, wk, wv):
@@ -172,7 +167,7 @@
     for c in range(total // step):
         at = slice(c * step, (c + 1) * step)
         bias = jnp.where(iota((step, 1), 0) + c * step < live, 0.0, masked_score)
-        project(xn[at, :], bias, at, wq, wk, wv, qs, ks, vs, head)
+        project(None, xn[at, :], bias, at, wq, wk, wv, qs, ks, vs, head)
 
     def query_tile(j, carry):
         cols = pl.ds(pl.multiple_of(j * 256, 256), 256)
@@ -206,30 +201,32 @@
 
 
 def tail_kernel(got, mid, gain, wout, w_in, w_out, result, ctx):
-    tokens, width = mid.shape
-    feats = tokens // 8
+    rows, width, feats = mid.shape
     t, p = iota((128, 192), 0), iota((128, 192), 1)
     low = onehot(p == (t & 15) * 12 + (t >> 4))
     high = onehot(p == (t & 15) * 12 + 8 + ((t >> 4) & 3))
     early = iota((128, 64), 0) < 64
+    wo = flipped(wout[...])
+    wi = w_in[...].T
     for b in range(feats // 16):
         a = got[b * 192 : (b + 1) * 192, :]
         hi = nn(high, a)
         lo = nn(low, a).astype(bf16)
         hi = jnp.where(early, hi[:, 0:64], hi[:, 64:128]).astype(bf16)
-        for r in range(8):
+        for r in range(rows):
             at = slice(r * feats + b * 16, r * feats + b * 16 + 16)
             ctx[at, 0:128] = lo[r * 16 : (r + 1) * 16]
             ctx[at, 128:width] = hi[r * 16 : (r + 1) * 16]
-    g2 = gain[2:3, :]
-    step = 256
-    for c in range(tokens // step):
-        at = slice(c * step, (c + 1) * step)
-        late = mid[at, :] + nn(ctx[at, :], wout[...])
+    g2 = jnp.broadcast_to(column(gain[2:3, :]), (width, 2 * feats))
+    for c in range(rows // 2):
+        old = jnp.concatenate([mid[2 * c], mid[2 * c + 1]], axis=1)
+        late = old + nt(wo, ctx[c * 2 * feats : (c + 1) * 2 * feats, :])
         n3 = layer_norm(late, g2).astype(bf16)
-        z = nn(n3, w_in[...])
+        z = nn(wi, n3)
         hidden = (z * 0.5 * (1.0 + lax.erf(z * math.sqrt(0.5)))).astype(bf16)
-        result[at, :] = late + nn(hidden, w_out[...])
+        out = late + nn(w_out[...], hidden)
+        result[2 * c] = out[:, 0:feats]
+        result[2 * c + 1] = out[:, feats : 2 * feats]
 
 
 def scratch(tokens, width):
@@ -251,11 +248,12 @@
 
 
 def front(present, cells, gain, qkv, wout):
-    tokens, width = cells.shape
+    rows, width, feats = cells.shape
+    tokens = rows * feats
     return pl.pallas_call(
         front_kernel,
         out_shape=(
-            jax.ShapeDtypeStruct((tokens, width), f32),
+            jax.ShapeDtypeStruct(cells.shape, f32),
             jax.ShapeDtypeStruct((tokens * width // 128, 128), bf16),
         ),
         in_specs=[VMEM] * 5,
@@ -279,12 +277,13 @@
 
 
 def tail(got, mid, gain, wout, w_in, w_out):
+    rows, width, feats = mid.shape
     return pl.pallas_call(
         tail_kernel,
         out_shape=jax.ShapeDtypeStruct(mid.shape, f32),
         in_specs=[VMEM] * 6,
         out_specs=VMEM,
-        scratch_shapes=[pltpu.VMEM(mid.shape, bf16)],
+        scratch_shapes=[pltpu.VMEM((rows * feats, width), bf16)],
         name="tail",
     )(got, mid, gain, wout, w_in, w_out)
 
@@ -298,14 +297,13 @@
 def body(
     cells, n_train, present, norm_gain, feat_qkv, feat_out, item_qkv, item_out, mlp_in, mlp_out
 ):
-    row_dev, feature_count, width = cells.shape
-    flat = cells.reshape(row_dev * feature_count, width)
-    mid, send = front(present.reshape(1, feature_count), flat, norm_gain, feat_qkv, feat_out)
+    stood = jnp.transpose(cells, (0, 2, 1))
+    mid, send = front(present.reshape(1, -1), stood, norm_gain, feat_qkv, feat_out)
     got = exchanged(send)
     back = rows(n_train, got, item_qkv)
     returned = exchanged(back)
-    out = tail(returned, mid, norm_gain, item_out, mlp_in, mlp_out)
-    return out.reshape(cells.shape)
+    out = tail(returned, mid, norm_gain, item_out, mlp_in, jnp.transpose(mlp_out))
+    return jnp.transpose(out, (0, 2, 1))
 
 
 def solution(mesh):

time: 125 us -> 118 us (0.944)
  blocking collectives: 0 us -> 35.4 us
  waiting for transfers between devices: 48.7 us -> 24.5 us
  starting transfers between devices: 41.2 us -> 31 us
  local copies, waits for them, and re-layouts: 7.35 us -> 0.75 us
    all_to_all x0 -> x1, blocking collectives: none -> 35.4 us  [exchanged(): return lax.all_to_all(tiles, ROW, 0, 0, tiled=True).reshape(block.shape)]
    all_to_all x2 -> x1, waiting for transfers between devices: 48.7 us -> 24.5 us  [exchanged(): return lax.all_to_all(tiles, ROW, 0, 0, tiled=True).reshape(block.shape)]
    all_to_all x2 -> x1, starting transfers between devices: 41.2 us -> 31 us  [exchanged(): return lax.all_to_all(tiles, ROW, 0, 0, tiled=True).reshape(block.shape)]
    unnamed x8 -> x2, local copies, waits for them, and re-layouts: 4.91 us -> 0.75 us
    reshape x1 -> x0, local copies, waits for them, and re-layouts: 2.44 us -> none  [body(): return out.reshape(cells.shape)]
  transfers between devices with their start and end apart: 2 -> 1, of which waited for: 2 -> 1; matrix products, arithmetic and copies ran while one was open for 1% -> 0% of each run, Pallas kernels for 0% -> 0%
where the time goes in v1:
time: 118 us
  blocking collectives  35.4 us (30%)
  starting transfers between devices  31 us (26%)
  Pallas kernels  25.6 us (22%)
  waiting for transfers between devices  24.5 us (21%)
    all_to_all x1, blocking collectives, exchanged(): return lax.all_to_all(tiles, ROW, 0, 0, tiled=True).reshape(block.shape)  35.4 us
    all_to_all x1, starting transfers between devices, exchanged(): return lax.all_to_all(tiles, ROW, 0, 0, tiled=True).reshape(block.shape)  31 us
    all_to_all x1, waiting for transfers between devices, exchanged(): return lax.all_to_all(tiles, ROW, 0, 0, tiled=True).reshape(block.shape)  24.5 us
    pallas_call x1, Pallas kernels, rows(): pl.pallas_call(rows_kernel, out_shape=jax.ShapeDtypeStruct(got.shape, bf1...  14.2 us
    pallas_call x1, Pallas kernels, front(): pl.pallas_call(front_kernel, out_shape=(jax.ShapeDtypeStruct(cells.shape,...  6.19 us
    pallas_call x1, Pallas kernels, tail(): pl.pallas_call(tail_kernel, out_shape=jax.ShapeDtypeStruct(mid.shape, f32...  5.13 us
  transfers between devices with their start and end apart: 1, of which 1 were waited for; matrix products, arithmetic and copies ran while one was open for 0% of the time, Pallas kernels for 0%

profile of v1, /device:TPU:33, one launch (start us, length us, event | category | flops | bytes accessed | tf_op | source)
XLA Modules:
  0.0 117.9 jit_solution(13592588693782587819)
XLA Ops:
  0.0 6.2 %front.1 = (f32[8,192,128]{2,1,0:T(8,128)}, bf16[1536,128]{1,0:T(8,128)(2,1)}) custom-call(s32[1,128]{1,0:T(1,128)} %bitcast.14, f32[8,192,128]{2,1,0:T(8,128)} %bitcast.11, f32[3,192]{1,0:T(4,128)} %gain.3, bf16[3,192,192]{2,1,0:T(8,128)(2,1)} %qkv.2, bf16[192,192]{1,0:T(8,128)(2,1)} %wout.2), custom_call_target="tpu_custom_call" | custom-call | tf_op jit(solution)/shard_map/front/pallas_call | solution.py:253
  6.2 31.0 %all-to-all-start = ((bf16[128,3,4,128]{3,2,1,0:T(4,128)(2,1)}), bf16[128,3,4,128]{3,2,1,0:T(4,128)(2,1)S(1)}, u32[]{:S(2)}, u32[]{:S(2)}) async-start(bf16[128,3,4,128]{3,2,1,0:T(4,128)(2,1)} %bitcast.12), calls=%async_computation | async-start | bytes 786432 | tf_op jit(solution)/shard_map/all_to_all | solution.py:294
  37.9 24.5 %all-to-all-done = bf16[128,3,4,128]{3,2,1,0:T(4,128)(2,1)S(1)} async-done(((bf16[128,3,4,128]{3,2,1,0:T(4,128)(2,1)}), bf16[128,3,4,128]{3,2,1,0:T(4,128)(2,1)S(1)}, u32[]{:S(2)}, u32[]{:S(2)}) %all-to-all-start) | async-done | bytes 393248 | tf_op jit(solution)/shard_map/all_to_all | solution.py:294
  62.4 0.0 copy-start
  62.4 0.7 copy-done
  63.1 14.2 %rows.1 = bf16[1536,128]{1,0:T(8,128)(2,1)} custom-call(s32[1]{0:T(128)S(6)} %copy.11.n_train, bf16[1536,128]{1,0:T(8,128)(2,1)} %bitcast.8, bf16[3,192,192]{2,1,0:T(8,128)(2,1)} %qkv.3), custom_call_target="tpu_custom_call" | custom-call | tf_op jit(solution)/shard_map/rows/pallas_call | solution.py:269
  77.4 35.4 %all_to_all.10 = bf16[128,3,4,128]{3,2,1,0:T(4,128)(2,1)} all-to-all(bf16[128,3,4,128]{3,2,1,0:T(4,128)(2,1)} %bitcast.9), channel_id=1, replica_groups=mesh['grp'=2,'row'=128] {'row'}, dimensions={0} | all-to-all | bytes 786432 | tf_op jit(solution)/shard_map/all_to_all | solution.py:294
  112.7 5.1 %tail.1 = f32[8,192,128]{2,1,0:T(8,128)} custom-call(bf16[1536,128]{1,0:T(8,128)(2,1)} %bitcast.10, f32[8,192,128]{2,1,0:T(8,128)} %get-tuple-element.8.mid, f32[3,192]{1,0:T(4,128)} %gain.3, bf16[192,192]{1,0:T(8,128)(2,1)} %wout.3, bf16[192,768]{1,0:T(8,128)(2,1)} %w_in.1, bf16[192,768]{1,0:T(8,128)(2,1)} %bitcast.13), custom_call_target="tpu_custom_call" | custom-call | tf_op jit(solution)/shard_map/tail/pallas_call | solution.py:281
Async XLA Ops:
  6.2 56.2 %all-to-all-start = ((bf16[128,3,4,128]{3,2,1,0:T(4,128)(2,1)}), bf16[128,3,4,128]{3,2,1,0:T(4,128)(2,1)S(1)}, u32[]{:S(2)}, u32[]{:S(2)}) async-start(bf16[128,3,4,128]{3,2,1,0:T(4,128)(2,1)} %bitcast.12), calls=%async_computation | async-start | bytes 786432 | tf_op jit(solution)/shard_map/all_to_all | solution.py:294
  62.4 0.7 copy-start

commit v2 on v1

--- a/solution.py
+++ b/solution.py
@@ -57,63 +57,61 @@
     return nt(eye, w).astype(bf16)
 
 
-def spread_keys(w, head):
-    n = w.shape[0]
-    shape = (n, HEADS * 128)
-    col = iota(shape, 1)
-    lane = col & 127
-    place = onehot((iota(shape, 0) == (col >> 7) * head + (lane & (head - 1))) & (lane < 3 * head))
-    return nn(w, place).astype(bf16)
-
-
-def prepare_weights(qkv, wq, wk, wv, head):
-    wq[...] = flipped(qkv[0])
-    wk[...] = spread_keys(qkv[1], head)
-    wv[...] = flipped(qkv[2])
+def prepare_weights(qkv, wt):
+    width = qkv.shape[-1]
+    for c in range(3):
+        wt[c * width : (c + 1) * width, :] = flipped(qkv[c])
 
 
 def fill_constant_rows(qs, vs, head):
+    cols = qs.shape[-1]
+    one_row = onehot(iota((head, cols), 0) == 0)
     for h in range(HEADS):
-        cols = qs.shape[-1]
-        one_row = onehot(iota((head, cols), 0) == 0)
         qs[h, 3 * head : 4 * head, :] = one_row
         vs[h, head : head + 16, :] = jnp.ones((16, cols), bf16)
 
 
-def project(xt, x, bias, rows, wq, wk, wv, qs, ks, vs, head):
+def split(v):
+    hi = v.astype(bf16)
+    return hi, (v - hi.astype(f32)).astype(bf16)
+
+
+def project(triple, bias, rows, qs, ks, vs, head):
+    width = triple.shape[0] // 3
     scale = (1.0 / math.sqrt(head)) * math.log2(math.e)
-    q = (nn(wq[...], xt) if xt is not None else nt(wq[...], x)) * scale
-    qh = q.astype(bf16)
-    ql = (q - qh.astype(f32)).astype(bf16)
-    v = (nn(wv[...], xt) if xt is not None else nt(wv[...], x)).astype(bf16)
+    qh, ql = split(triple[0:width] * scale)
+    kh, kl = split(triple[width : 2 * width])
+    v = triple[2 * width : 3 * width].astype(bf16)
+    shape = (head, triple.shape[1])
+    last = jnp.where(iota(shape, 0) == 0, bias, 0.0).astype(bf16)
     for h in range(HEADS):
         mine = slice(h * head, (h + 1) * head)
         qs[h, 0:head, rows] = qh[mine]
         qs[h, head : 2 * head, rows] = ql[mine]
         qs[h, 2 * head : 3 * head, rows] = qh[mine]
         vs[h, 0:head, rows] = v[mine]
-    lane = iota((x.shape[0], 128), 1)
-    for h in range(HEADS):
-        k = nn(x, wk[:, h * 128 : (h + 1) * 128])
-        kh = k.astype(bf16).astype(f32)
-        kl = k - kh
-        packed = jnp.where(lane < 2 * head, kh, jnp.where(lane < 3 * head, kl, bias))
-        ks[rows, h * 128 : (h + 1) * 128] = packed.astype(bf16)
-
-
-def front_kernel(present, cells, gain, qkv, wout, mid, send, xn, qs, ks, vs, ctx, wq, wk, wv):
+        stack = jnp.concatenate([kh[mine], kh[mine], kl[mine], last], axis=0)
+        ks[rows, h * 128 : (h + 1) * 128] = stack.T
+
+
+def front_kernel(present, cells, gain, qkv, wout, mid, send, xn, qs, ks, vs, ctx, wt, raw, sems):
     rows, width, feats = cells.shape
     head = width // HEADS
-    prepare_weights(qkv, wq, wk, wv, head)
+    copies = [pltpu.make_async_copy(cells.at[r], raw.at[r], sems.at[r]) for r in range(rows)]
+    for c in copies:
+        c.start()
+    prepare_weights(qkv, wt)
     wo = flipped(wout[...])
     fill_constant_rows(qs, vs, head)
     g0 = jnp.broadcast_to(column(gain[0:1, :]), (width, feats))
     g1 = jnp.broadcast_to(column(gain[1:2, :]), (width, feats))
-    bias = column(jnp.where(present[...] > 0, 0.0, masked_score))
-    bias = jnp.concatenate([bias, bias], axis=0)
+    bias = jnp.where(present[...] > 0, 0.0, masked_score)
+    bias = jnp.concatenate([bias, bias], axis=1)
     for c in range(rows // 2):
-        xt = jnp.concatenate([layer_norm(cells[2 * c + k], g0).astype(bf16) for k in range(2)], axis=1)
-        project(xt, xt.T, bias, slice(c * 2 * feats, (c + 1) * 2 * feats), wq, wk, wv, qs, ks, vs, head)
+        copies[2 * c].wait()
+        copies[2 * c + 1].wait()
+        xt = jnp.concatenate([layer_norm(raw[2 * c + k], g0).astype(bf16) for k in range(2)], axis=1)
+        project(nn(wt[...], xt), bias, slice(c * 2 * feats, (c + 1) * 2 * feats), qs, ks, vs, head)
     for r in range(rows):
         at = slice(r * feats, (r + 1) * feats)
         scores = [nn(ks[at, h * 128 : (h + 1) * 128], qs[h, :, at]) for h in range(HEADS)]
@@ -128,7 +126,7 @@
         both = nn(wo, ctx[:, c * 2 * feats : (c + 1) * 2 * feats])
         for k in range(2):
             r = 2 * c + k
-            m = cells[r] + both[:, k * feats : (k + 1) * feats]
+            m = raw[r] + both[:, k * feats : (k + 1) * feats]
             mid[r] = m
             xn[r * feats : (r + 1) * feats, :] = layer_norm(m, g1).astype(bf16).T
     shape = (192, rows * 16)
@@ -147,11 +145,11 @@
         send[b * 192 : (b + 1) * 192, :] = out.astype(bf16)
 
 
-def rows_kernel(n_train, got, qkv, send, xn, qs, ks, vs, ctx, wq, wk, wv):
+def rows_kernel(n_train, got, qkv, send, xn, qs, ks, vs, ctx, wt, sbuf):
     width = qkv.shape[-1]
     head = width // HEADS
     total = xn.shape[0]
-    prepare_weights(qkv, wq, wk, wv, head)
+    prepare_weights(qkv, wt)
     fill_constant_rows(qs, vs, head)
     t, p = iota((128, 192), 0), iota((128, 192), 1)
     low = onehot(p == (t >> 3) * 12 + (t & 7))
@@ -166,26 +164,41 @@
     step = 256
     for c in range(total // step):
         at = slice(c * step, (c + 1) * step)
-        bias = jnp.where(iota((step, 1), 0) + c * step < live, 0.0, masked_score)
-        project(None, xn[at, :], bias, at, wq, wk, wv, qs, ks, vs, head)
-
-    def query_tile(j, carry):
-        cols = pl.ds(pl.multiple_of(j * 256, 256), 256)
-
-        def score(h):
-            return nn(ks[:, h * 128 : (h + 1) * 128], qs[h, :, cols])
-
-        s = score(0)
+        bias = jnp.where(iota((1, step), 1) + c * step < live, 0.0, masked_score)
+        project(nt(wt[...], xn[at, :]), bias, at, qs, ks, vs, head)
+
+    tiles = total // 256
+    blocks = total // 256
+
+    def score(h, cols, b):
+        s = nn(ks[b * 256 : (b + 1) * 256, h * 128 : (h + 1) * 128], qs[h, :, cols])
+        sbuf[h % 2, b * 256 : (b + 1) * 256, :] = s
+        return jnp.max(s.reshape(32, 8, 256), axis=0)
+
+    def columns(j):
+        return pl.ds(pl.multiple_of(j * 256, 256), 256)
+
+    peak = score(0, slice(0, 256), 0)
+    for b in range(1, blocks):
+        peak = jnp.maximum(peak, score(0, slice(0, 256), b))
+
+    def query_tile(j, peak):
+        cols = columns(j)
+        after = columns(jnp.minimum(j + 1, tiles - 1))
         for h in range(HEADS):
-            ahead = score(h + 1) if h + 1 < HEADS else None
-            top = jnp.max(s, axis=0, keepdims=True)
-            w = jnp.exp2(s - top).astype(bf16)
-            o = nn(vs[h], w)
+            top = jnp.max(peak, axis=0, keepdims=True)
+            o = None
+            peak = None
+            for b in range(blocks):
+                ahead = score(h + 1, cols, b) if h + 1 < HEADS else score(0, after, b)
+                peak = ahead if peak is None else jnp.maximum(peak, ahead)
+                w = jnp.exp2(sbuf[h % 2, b * 256 : (b + 1) * 256, :] - top).astype(bf16)
+                part = nn(vs[h, :, b * 256 : (b + 1) * 256], w)
+                o = part if o is None else o + part
             ctx[h * head : (h + 1) * head, cols] = (o[0:head] * (1.0 / o[head : head + 1])).astype(bf16)
-            s = ahead
-        return carry
-
-    lax.fori_loop(0, total // 256, query_tile, 0)
+        return peak
+
+    lax.fori_loop(0, tiles, query_tile, peak)
     o, q = iota((192, 128), 0), iota((192, 128), 1)
     base, r = (q >> 3) * 12, q & 7
     low = onehot(o == base + r)
@@ -200,7 +213,7 @@
         send[b * 192 : (b + 1) * 192, :] = out.astype(bf16)
 
 
-def tail_kernel(got, mid, gain, wout, w_in, w_out, result, ctx):
+def tail_kernel(got, mid, gain, wout, w_in, w_out, result, ctx, out_buf, sems):
     rows, width, feats = mid.shape
     t, p = iota((128, 192), 0), iota((128, 192), 1)
     low = onehot(p == (t & 15) * 12 + (t >> 4))
@@ -218,6 +231,7 @@
             ctx[at, 0:128] = lo[r * 16 : (r + 1) * 16]
             ctx[at, 128:width] = hi[r * 16 : (r + 1) * 16]
     g2 = jnp.broadcast_to(column(gain[2:3, :]), (width, 2 * feats))
+    sent = []
     for c in range(rows // 2):
         old = jnp.concatenate([mid[2 * c], mid[2 * c + 1]], axis=1)
         late = old + nt(wo, ctx[c * 2 * feats : (c + 1) * 2 * feats, :])
@@ -225,8 +239,12 @@
         z = nn(wi, n3)
         hidden = (z * 0.5 * (1.0 + lax.erf(z * math.sqrt(0.5)))).astype(bf16)
         out = late + nn(w_out[...], hidden)
-        result[2 * c] = out[:, 0:feats]
-        result[2 * c + 1] = out[:, feats : 2 * feats]
+        for k in range(2):
+            out_buf[2 * c + k] = out[:, k * feats : (k + 1) * feats]
+            sent.append(pltpu.make_async_copy(out_buf.at[2 * c + k], result.at[2 * c + k], sems.at[2 * c + k]))
+            sent[-1].start()
+    for s in sent:
+        s.wait()
 
 
 def scratch(tokens, width):
@@ -237,14 +255,17 @@
         pltpu.VMEM((tokens, HEADS * 128), bf16),
         pltpu.VMEM((HEADS, head + 16, tokens), bf16),
         pltpu.VMEM((width, tokens), bf16),
-        pltpu.VMEM((width, width), bf16),
-        pltpu.VMEM((width, HEADS * 128), bf16),
-        pltpu.VMEM((width, width), bf16),
+        pltpu.VMEM((3 * width, width), bf16),
     ]
 
 
 VMEM = pl.BlockSpec(memory_space=pltpu.VMEM)
 SMEM = pl.BlockSpec(memory_space=pltpu.SMEM)
+ANY = pl.BlockSpec(memory_space=pl.ANY)
+
+
+def near(x):
+    return pltpu.with_memory_space_constraint(x, pltpu.VMEM)
 
 
 def front(present, cells, gain, qkv, wout):
@@ -253,12 +274,12 @@
     return pl.pallas_call(
         front_kernel,
         out_shape=(
-            jax.ShapeDtypeStruct(cells.shape, f32),
-            jax.ShapeDtypeStruct((tokens * width // 128, 128), bf16),
+            pltpu.VMEM(cells.shape, f32),
+            pltpu.VMEM((tokens * width // 128, 128), bf16),
         ),
-        in_specs=[VMEM] * 5,
+        in_specs=[VMEM, ANY, VMEM, VMEM, VMEM],
         out_specs=(VMEM, VMEM),
-        scratch_shapes=scratch(tokens, width),
+        scratch_shapes=[*scratch(tokens, width), pltpu.VMEM(cells.shape, f32), pltpu.SemaphoreType.DMA((rows,))],
         name="front",
     )(present, cells, gain, qkv, wout)
 
@@ -268,12 +289,12 @@
     tokens = got.shape[0] * 128 // width
     return pl.pallas_call(
         rows_kernel,
-        out_shape=jax.ShapeDtypeStruct(got.shape, bf16),
+        out_shape=pltpu.VMEM(got.shape, bf16),
         in_specs=[SMEM, VMEM, VMEM],
         out_specs=VMEM,
-        scratch_shapes=scratch(tokens, width),
+        scratch_shapes=[*scratch(tokens, width), pltpu.VMEM((2, tokens, 256), f32)],
         name="rows",
-    )(n_train, got, qkv)
+    )(n_train, near(got), near(qkv))
 
 
 def tail(got, mid, gain, wout, w_in, w_out):
@@ -282,10 +303,14 @@
         tail_kernel,
         out_shape=jax.ShapeDtypeStruct(mid.shape, f32),
         in_specs=[VMEM] * 6,
-        out_specs=VMEM,
-        scratch_shapes=[pltpu.VMEM((rows * feats, width), bf16)],
+        out_specs=ANY,
+        scratch_shapes=[
+            pltpu.VMEM((rows * feats, width), bf16),
+            pltpu.VMEM(mid.shape, f32),
+            pltpu.SemaphoreType.DMA((rows,)),
+        ],
         name="tail",
-    )(got, mid, gain, wout, w_in, w_out)
+    )(near(got), near(mid), near(gain), near(wout), near(w_in), near(w_out))
 
 
 def exchanged(block):

time: 118 us -> 113 us (0.958)
  Pallas kernels: 25.6 us -> 20.6 us
    pallas_call x2, Pallas kernels: 20.4 us -> 17.1 us  [the longest x1 9.9 us: rows(): pl.pallas_call(rows_kernel, out_shape=pltpu.VMEM(got.shape, bf16), in_spe...]
    pallas_call x1, Pallas kernels: 5.13 us -> 3.55 us  [tail(): pl.pallas_call(tail_kernel, out_shape=jax.ShapeDtypeStruct(mid.shape, f32...]
where the time goes in v2:
time: 113 us
  blocking collectives  35.2 us (31%)
  starting transfers between devices  31.1 us (28%)
  waiting for transfers between devices  24.5 us (22%)
  Pallas kernels  20.6 us (18%)
    all_to_all x1, blocking collectives, exchanged(): return lax.all_to_all(tiles, ROW, 0, 0, tiled=True).reshape(block.shape)  35.2 us
    all_to_all x1, starting transfers between devices, exchanged(): return lax.all_to_all(tiles, ROW, 0, 0, tiled=True).reshape(block.shape)  31.1 us
    all_to_all x1, waiting for transfers between devices, exchanged(): return lax.all_to_all(tiles, ROW, 0, 0, tiled=True).reshape(block.shape)  24.5 us
    pallas_call x1, Pallas kernels, rows(): pl.pallas_call(rows_kernel, out_shape=pltpu.VMEM(got.shape, bf16), in_spe...  9.9 us
    pallas_call x1, Pallas kernels, front(): pl.pallas_call(front_kernel, out_shape=(pltpu.VMEM(cells.shape, f32), plt...  7.17 us
    pallas_call x1, Pallas kernels, tail(): pl.pallas_call(tail_kernel, out_shape=jax.ShapeDtypeStruct(mid.shape, f32...  3.55 us
  transfers between devices with their start and end apart: 1, of which 1 were waited for; matrix products, arithmetic and copies ran while one was open for 0% of the time, Pallas kernels for 0%

profile of v2, /device:TPU:33, one launch (start us, length us, event | category | flops | bytes accessed | tf_op | source)
XLA Modules:
  0.0 113.0 jit_solution(11642411598477748485)
XLA Ops:
  0.0 7.2 %front.1 = (f32[8,192,128]{2,1,0:T(8,128)S(1)}, bf16[1536,128]{1,0:T(8,128)(2,1)}) custom-call(s32[1,128]{1,0:T(1,128)} %bitcast.13, f32[8,192,128]{2,1,0:T(8,128)} %bitcast.12, f32[3,192]{1,0:T(4,128)} %gain.3, bf16[3,192,192]{2,1,0:T(8,128)(2,1)} %qkv.2, bf16[192,192]{1,0:T(8,128)(2,1)} %wout.2), custom_call_target="tpu_custom_call" | custom-call | tf_op jit(solution)/shard_map/front/pallas_call | solution.py:274
  7.2 0.0 copy-start
  7.2 31.1 %all-to-all-start = ((bf16[128,3,4,128]{3,2,1,0:T(4,128)(2,1)}), bf16[128,3,4,128]{3,2,1,0:T(4,128)(2,1)S(1)}, u32[]{:S(2)}, u32[]{:S(2)}) async-start(bf16[128,3,4,128]{3,2,1,0:T(4,128)(2,1)} %bitcast.2), calls=%async_computation | async-start | bytes 786432 | tf_op jit(solution)/shard_map/all_to_all | solution.py:319
  39.0 24.5 %all-to-all-done = bf16[128,3,4,128]{3,2,1,0:T(4,128)(2,1)S(1)} async-done(((bf16[128,3,4,128]{3,2,1,0:T(4,128)(2,1)}), bf16[128,3,4,128]{3,2,1,0:T(4,128)(2,1)S(1)}, u32[]{:S(2)}, u32[]{:S(2)}) %all-to-all-start) | async-done | bytes 393248 | tf_op jit(solution)/shard_map/all_to_all | solution.py:319
  63.5 0.0 copy-done
  63.5 9.9 %rows.1 = bf16[1536,128]{1,0:T(8,128)(2,1)S(1)} custom-call(s32[1]{0:T(128)S(6)} %copy.11.n_train, bf16[1536,128]{1,0:T(8,128)(2,1)S(1)} %bitcast.8, bf16[3,192,192]{2,1,0:T(8,128)(2,1)S(1)} %copy-done), custom_call_target="tpu_custom_call" | custom-call | tf_op jit(solution)/shard_map/rows/pallas_call | solution.py:290
  73.4 0.0 copy-start.1
  73.4 0.0 copy-start.2
  73.4 0.0 copy-start.3
  73.4 35.2 %all_to_all.10 = bf16[128,3,4,128]{3,2,1,0:T(4,128)(2,1)S(1)} all-to-all(bf16[128,3,4,128]{3,2,1,0:T(4,128)(2,1)S(1)} %bitcast.9), channel_id=1, replica_groups=mesh['grp'=2,'row'=128] {'row'}, dimensions={0} | all-to-all | bytes 786432 | tf_op jit(solution)/shard_map/all_to_all | solution.py:319
  108.6 0.0 copy-start.4
  108.6 0.0 copy-done.1
  108.6 0.0 copy-done.2
  108.6 0.0 copy-done.3
  108.6 0.7 copy-done.4
  109.3 3.6 %tail.1 = f32[8,192,128]{2,1,0:T(8,128)} custom-call(bf16[1536,128]{1,0:T(8,128)(2,1)S(1)} %bitcast.10, f32[8,192,128]{2,1,0:T(8,128)S(1)} %get-tuple-element.8.mid, f32[3,192]{1,0:T(4,128)S(1)} %copy-done.4, bf16[192,192]{1,0:T(8,128)(2,1)S(1)} %copy-done.3, bf16[192,768]{1,0:T(8,128)(2,1)S(1)} %copy-done.1, bf16[192,768]{1,0:T(8,128)(2,1)S(1)} %bitcast.11), custom_call_target="tpu_custom_call" | custom-call | tf_op jit(solution)/shard_map/tail/pallas_call | solution.py:302
Async XLA Ops:
  7.2 56.3 %copy-start = (bf16[3,192,192]{2,1,0:T(8,128)(2,1)S(1)}, bf16[3,192,192]{2,1,0:T(8,128)(2,1)}, u32[]{:S(2)}) copy-start(bf16[3,192,192]{2,1,0:T(8,128)(2,1)} %qkv.3) | copy-start | bytes 663556
  7.2 56.3 %all-to-all-start = ((bf16[128,3,4,128]{3,2,1,0:T(4,128)(2,1)}), bf16[128,3,4,128]{3,2,1,0:T(4,128)(2,1)S(1)}, u32[]{:S(2)}, u32[]{:S(2)}) async-start(bf16[128,3,4,128]{3,2,1,0:T(4,128)(2,1)} %bitcast.2), calls=%async_computation | async-start | bytes 786432 | tf_op jit(solution)/shard_map/all_to_all | solution.py:319
  73.4 35.2 %copy-start.1 = (bf16[192,768]{1,0:T(8,128)(2,1)S(1)}, bf16[192,768]{1,0:T(8,128)(2,1)}, u32[]{:S(2)}) copy-start(bf16[192,768]{1,0:T(8,128)(2,1)} %w_in.1) | copy-start | bytes 884740
  73.4 35.2 %copy-start.2 = (bf16[768,192]{0,1:T(8,128)(2,1)S(1)}, bf16[768,192]{0,1:T(8,128)(2,1)}, u32[]{:S(2)}) copy-start(bf16[768,192]{0,1:T(8,128)(2,1)} %param.19) | copy-start | bytes 884740
  73.4 35.2 %copy-start.3 = (bf16[192,192]{1,0:T(8,128)(2,1)S(1)}, bf16[192,192]{1,0:T(8,128)(2,1)}, u32[]{:S(2)}) copy-start(bf16[192,192]{1,0:T(8,128)(2,1)} %wout.3) | copy-start | bytes 221188
  108.6 0.7 copy-start.4

commit v3 on v2

--- a/solution.py
+++ b/solution.py
@@ -51,16 +51,10 @@
     return jnp.sum(jnp.where(eye, row, 0.0), axis=1, keepdims=True)
 
 
-def flipped(w):
-    n = w.shape[0]
-    eye = onehot(iota((n, n), 0) == iota((n, n), 1))
-    return nt(eye, w).astype(bf16)
-
-
 def prepare_weights(qkv, wt):
     width = qkv.shape[-1]
     for c in range(3):
-        wt[c * width : (c + 1) * width, :] = flipped(qkv[c])
+        wt[c * width : (c + 1) * width, :] = qkv[c].T
 
 
 def fill_constant_rows(qs, vs, head):
@@ -94,62 +88,136 @@
         ks[rows, h * 128 : (h + 1) * 128] = stack.T
 
 
-def front_kernel(present, cells, gain, qkv, wout, mid, send, xn, qs, ks, vs, ctx, wt, raw, sems):
+def front_kernel(
+    present, cells, gain, qkv, wout, mid, send, raw, wq, wo, xn, qs, ks, vs, ctx, wt, cell_sems, sems
+):
     rows, width, feats = cells.shape
     head = width // HEADS
-    copies = [pltpu.make_async_copy(cells.at[r], raw.at[r], sems.at[r]) for r in range(rows)]
-    for c in copies:
+    step = 2 * feats
+    chunks = rows // 2
+    copies = [pltpu.make_async_copy(cells.at[r], raw.at[r], cell_sems.at[r]) for r in range(rows)]
+    first = pltpu.make_async_copy(qkv, wq, sems.at[0])
+    second = pltpu.make_async_copy(wout, wo, sems.at[1])
+    copies[0].start()
+    copies[1].start()
+    first.start()
+    for c in copies[2:]:
         c.start()
-    prepare_weights(qkv, wt)
-    wo = flipped(wout[...])
-    fill_constant_rows(qs, vs, head)
+    second.start()
+    for p in range(HEADS // 2):
+        for r in range(rows):
+            qs[p, 0:128, r * step + feats : (r + 1) * step] = jnp.zeros((128, feats), bf16)
+            qs[p, 128:256, r * step : r * step + feats] = jnp.zeros((128, feats), bf16)
+            one_row = onehot(iota((head, feats), 0) == 0)
+            qs[p, 3 * head : 4 * head, r * step : r * step + feats] = one_row
+            qs[p, 7 * head : 8 * head, r * step + feats : (r + 1) * step] = one_row
+    for h in range(HEADS):
+        at = h * (head + 16) + head
+        vs[at : at + 16, :] = jnp.ones((16, rows * feats), bf16)
     g0 = jnp.broadcast_to(column(gain[0:1, :]), (width, feats))
     g1 = jnp.broadcast_to(column(gain[1:2, :]), (width, feats))
     bias = jnp.where(present[...] > 0, 0.0, masked_score)
     bias = jnp.concatenate([bias, bias], axis=1)
-    for c in range(rows // 2):
+    last = jnp.where(iota((head, step), 0) == 0, bias, 0.0).astype(bf16)
+    first.wait()
+    prepare_weights(wq, wt)
+    scale = (1.0 / math.sqrt(head)) * math.log2(math.e)
+
+    def normed(c):
         copies[2 * c].wait()
         copies[2 * c + 1].wait()
-        xt = jnp.concatenate([layer_norm(raw[2 * c + k], g0).astype(bf16) for k in range(2)], axis=1)
-        project(nn(wt[...], xt), bias, slice(c * 2 * feats, (c + 1) * 2 * feats), qs, ks, vs, head)
+        return jnp.concatenate([layer_norm(raw[2 * c + k], g0).astype(bf16) for k in range(2)], axis=1)
+
+    def place(c, triple):
+        tok = slice(c * step, (c + 1) * step)
+        qh, ql = split(triple[0:width] * scale)
+        kh, kl = split(triple[width : 2 * width])
+        v = triple[2 * width : 3 * width].astype(bf16)
+        for h in range(HEADS):
+            mine = slice(h * head, (h + 1) * head)
+            vs[h * (head + 16) : h * (head + 16) + head, tok] = v[mine]
+            up = (h % 2) * 128
+            for k in range(2):
+                col = (2 * c + k) * step + (h % 2) * feats
+                part = slice(k * feats, (k + 1) * feats)
+                qs[h // 2, up : up + head, col : col + feats] = qh[mine, part]
+                qs[h // 2, up + head : up + 2 * head, col : col + feats] = ql[mine, part]
+                qs[h // 2, up + 2 * head : up + 3 * head, col : col + feats] = qh[mine, part]
+            ks[tok, h * 128 : (h + 1) * 128] = jnp.concatenate([kh[mine], kh[mine], kl[mine], last], axis=0).T
+
+    xt = normed(0)
+    triple = nn(wt[...], xt)
+    for c in range(chunks):
+        if c + 1 < chunks:
+            ahead = nn(wt[...], normed(c + 1))
+        place(c, triple)
+        triple = ahead
+
+    def scores(r):
+        at = slice(r * feats, (r + 1) * feats)
+        return [nn(ks[at, p * 256 : (p + 1) * 256], qs[p, :, r * step : (r + 1) * step]) for p in range(HEADS // 2)]
+
+    def attend(r, s):
+        at = slice(r * feats, (r + 1) * feats)
+        w = [jnp.exp2(x - jnp.max(x, axis=0, keepdims=True)).astype(bf16) for x in s]
+        for p in range(HEADS // 2):
+            o = nn(vs[p * 2 * (head + 16) : (p + 1) * 2 * (head + 16), at], w[p])
+            for k in range(2):
+                lane, row = slice(k * feats, (k + 1) * feats), k * (head + 16)
+                h = 2 * p + k
+                inverse = 1.0 / o[row + head : row + head + 1, lane]
+                ctx[h * head : (h + 1) * head, at] = (o[row : row + head, lane] * inverse).astype(bf16)
+
+    s = scores(0)
     for r in range(rows):
-        at = slice(r * feats, (r + 1) * feats)
-        scores = [nn(ks[at, h * 128 : (h + 1) * 128], qs[h, :, at]) for h in range(HEADS)]
-        weights = []
-        for s in scores:
-            top = jnp.max(s, axis=0, keepdims=True)
-            weights.append(jnp.exp2(s - top).astype(bf16))
-        for h in range(HEADS):
-            o = nn(vs[h, :, at], weights[h])
-            ctx[h * head : (h + 1) * head, at] = (o[0:head] * (1.0 / o[head : head + 1])).astype(bf16)
-    for c in range(rows // 2):
-        both = nn(wo, ctx[:, c * 2 * feats : (c + 1) * 2 * feats])
+        if r + 1 < rows:
+            ahead = scores(r + 1)
+        attend(r, s)
+        s = ahead
+    second.wait()
+    wot = wo[...].T
+
+    def close(c, both):
         for k in range(2):
             r = 2 * c + k
             m = raw[r] + both[:, k * feats : (k + 1) * feats]
             mid[r] = m
             xn[r * feats : (r + 1) * feats, :] = layer_norm(m, g1).astype(bf16).T
+
+    both = nn(wot, ctx[:, 0:step])
+    for c in range(chunks):
+        if c + 1 < chunks:
+            ahead = nn(wot, ctx[:, (c + 1) * step : (c + 2) * step])
+        close(c, both)
+        both = ahead
     shape = (192, rows * 16)
     o, t = iota(shape, 0), iota(shape, 1)
     f, r = t & 15, t >> 4
     base = f * 12
     low = onehot(o == base + r)
-    first = onehot((o == base + 8 + (r & 3)) & (r < 4))
-    second = onehot((o == base + 8 + (r & 3)) & (r >= 4))
+    first_half = onehot((o == base + 8 + (r & 3)) & (r < 4))
+    second_half = onehot((o == base + 8 + (r & 3)) & (r >= 4))
     lane = iota((192, 128), 1)
     for b in range(feats // 16):
         x = jnp.concatenate([xn[k * feats + b * 16 : k * feats + b * 16 + 16, :] for k in range(rows)], axis=0)
         tail = x[:, 128:width]
         tails = jnp.concatenate([tail, tail], axis=1)
-        out = nn(low, x[:, 0:128]) + jnp.where(lane < 64, nn(first, tails), nn(second, tails))
+        out = nn(low, x[:, 0:128]) + jnp.where(lane < 64, nn(first_half, tails), nn(second_half, tails))
         send[b * 192 : (b + 1) * 192, :] = out.astype(bf16)
 
 
-def rows_kernel(n_train, got, qkv, send, xn, qs, ks, vs, ctx, wt, sbuf):
-    width = qkv.shape[-1]
+def prep_kernel(after, qkv, wout, w_in, gain, wt, wo, wi, g2):
+    del after
+    prepare_weights(qkv, wt)
+    wo[...] = wout[...].T
+    wi[...] = w_in[...].T
+    g2[...] = jnp.broadcast_to(column(gain[2:3, :]), g2.shape)
+
+
+def rows_kernel(n_train, got, wt, send, xn, qs, ks, vs, ctx, sbuf):
+    width = wt.shape[-1]
     head = width // HEADS
     total = xn.shape[0]
-    prepare_weights(qkv, wt)
     fill_constant_rows(qs, vs, head)
     t, p = iota((128, 192), 0), iota((128, 192), 1)
     low = onehot(p == (t >> 3) * 12 + (t & 7))
@@ -213,14 +281,12 @@
         send[b * 192 : (b + 1) * 192, :] = out.astype(bf16)
 
 
-def tail_kernel(got, mid, gain, wout, w_in, w_out, result, ctx, out_buf, sems):
+def tail_kernel(got, mid, g2, wo, wi, w_out, result, ctx, out_buf, sems):
     rows, width, feats = mid.shape
     t, p = iota((128, 192), 0), iota((128, 192), 1)
     low = onehot(p == (t & 15) * 12 + (t >> 4))
     high = onehot(p == (t & 15) * 12 + 8 + ((t >> 4) & 3))
     early = iota((128, 64), 0) < 64
-    wo = flipped(wout[...])
-    wi = w_in[...].T
     for b in range(feats // 16):
         a = got[b * 192 : (b + 1) * 192, :]
         hi = nn(high, a)
@@ -230,13 +296,12 @@
             at = slice(r * feats + b * 16, r * feats + b * 16 + 16)
             ctx[at, 0:128] = lo[r * 16 : (r + 1) * 16]
             ctx[at, 128:width] = hi[r * 16 : (r + 1) * 16]
-    g2 = jnp.broadcast_to(column(gain[2:3, :]), (width, 2 * feats))
     sent = []
     for c in range(rows // 2):
         old = jnp.concatenate([mid[2 * c], mid[2 * c + 1]], axis=1)
-        late = old + nt(wo, ctx[c * 2 * feats : (c + 1) * 2 * feats, :])
-        n3 = layer_norm(late, g2).astype(bf16)
-        z = nn(wi, n3)
+        late = old + nt(wo[...], ctx[c * 2 * feats : (c + 1) * 2 * feats, :])
+        n3 = layer_norm(late, g2[...]).astype(bf16)
+        z = nn(wi[...], n3)
         hidden = (z * 0.5 * (1.0 + lax.erf(z * math.sqrt(0.5)))).astype(bf16)
         out = late + nn(w_out[...], hidden)
         for k in range(2):
@@ -247,18 +312,6 @@
         s.wait()
 
 
-def scratch(tokens, width):
-    head = width // HEADS
-    return [
-        pltpu.VMEM((tokens, width), bf16),
-        pltpu.VMEM((HEADS, 4 * head, tokens), bf16),
-        pltpu.VMEM((tokens, HEADS * 128), bf16),
-        pltpu.VMEM((HEADS, head + 16, tokens), bf16),
-        pltpu.VMEM((width, tokens), bf16),
-        pltpu.VMEM((3 * width, width), bf16),
-    ]
-
-
 VMEM = pl.BlockSpec(memory_space=pltpu.VMEM)
 SMEM = pl.BlockSpec(memory_space=pltpu.SMEM)
 ANY = pl.BlockSpec(memory_space=pl.ANY)
@@ -270,6 +323,7 @@
 
 def front(present, cells, gain, qkv, wout):
     rows, width, feats = cells.shape
+    head = width // HEADS
     tokens = rows * feats
     return pl.pallas_call(
         front_kernel,
@@ -277,27 +331,63 @@
             pltpu.VMEM(cells.shape, f32),
             pltpu.VMEM((tokens * width // 128, 128), bf16),
         ),
-        in_specs=[VMEM, ANY, VMEM, VMEM, VMEM],
+        in_specs=[VMEM, ANY, VMEM, ANY, ANY],
         out_specs=(VMEM, VMEM),
-        scratch_shapes=[*scratch(tokens, width), pltpu.VMEM(cells.shape, f32), pltpu.SemaphoreType.DMA((rows,))],
+        scratch_shapes=[
+            pltpu.VMEM(cells.shape, f32),
+            pltpu.VMEM(qkv.shape, bf16),
+            pltpu.VMEM(wout.shape, bf16),
+            pltpu.VMEM((tokens, width), bf16),
+            pltpu.VMEM((HEADS // 2, 8 * head, 2 * tokens), bf16),
+            pltpu.VMEM((tokens, HEADS * 128), bf16),
+            pltpu.VMEM((HEADS * (head + 16), tokens), bf16),
+            pltpu.VMEM((width, tokens), bf16),
+            pltpu.VMEM((3 * width, width), bf16),
+            pltpu.SemaphoreType.DMA((rows,)),
+            pltpu.SemaphoreType.DMA((2,)),
+        ],
         name="front",
     )(present, cells, gain, qkv, wout)
 
 
-def rows(n_train, got, qkv):
-    width = qkv.shape[-1]
+def prep(after, qkv, wout, w_in, gain):
+    width, hidden = w_in.shape
+    return pl.pallas_call(
+        prep_kernel,
+        out_shape=(
+            pltpu.VMEM((3 * width, width), bf16),
+            pltpu.VMEM((width, width), bf16),
+            pltpu.VMEM((hidden, width), bf16),
+            pltpu.VMEM((width, 256), f32),
+        ),
+        in_specs=[VMEM] * 5,
+        out_specs=(VMEM, VMEM, VMEM, VMEM),
+        name="prep",
+    )(near(after), qkv, wout, w_in, gain)
+
+
+def rows(n_train, got, wt):
+    width = wt.shape[-1]
+    head = width // HEADS
     tokens = got.shape[0] * 128 // width
     return pl.pallas_call(
         rows_kernel,
         out_shape=pltpu.VMEM(got.shape, bf16),
         in_specs=[SMEM, VMEM, VMEM],
         out_specs=VMEM,
-        scratch_shapes=[*scratch(tokens, width), pltpu.VMEM((2, tokens, 256), f32)],
+        scratch_shapes=[
+            pltpu.VMEM((tokens, width), bf16),
+            pltpu.VMEM((HEADS, 4 * head, tokens), bf16),
+            pltpu.VMEM((tokens, HEADS * 128), bf16),
+            pltpu.VMEM((HEADS, head + 16, tokens), bf16),
+            pltpu.VMEM((width, tokens), bf16),
+            pltpu.VMEM((2, tokens, 256), f32),
+        ],
         name="rows",
-    )(n_train, near(got), near(qkv))
-
-
-def tail(got, mid, gain, wout, w_in, w_out):
+    )(n_train, near(got), near(wt))
+
+
+def tail(got, mid, g2, wo, wi, w_out):
     rows, width, feats = mid.shape
     return pl.pallas_call(
         tail_kernel,
@@ -310,7 +400,7 @@
             pltpu.SemaphoreType.DMA((rows,)),
         ],
         name="tail",
-    )(near(got), near(mid), near(gain), near(wout), near(w_in), near(w_out))
+    )(near(got), near(mid), near(g2), near(wo), near(wi), near(w_out))
 
 
 def exchanged(block):
@@ -324,10 +414,11 @@
 ):
     stood = jnp.transpose(cells, (0, 2, 1))
     mid, send = front(present.reshape(1, -1), stood, norm_gain, feat_qkv, feat_out)
+    wt, wo, wi, g2 = prep(mid, item_qkv, item_out, mlp_in, norm_gain)
     got = exchanged(send)
-    back = rows(n_train, got, item_qkv)
+    back = rows(n_train, got, wt)
     returned = exchanged(back)
-    out = tail(returned, mid, norm_gain, item_out, mlp_in, jnp.transpose(mlp_out))
+    out = tail(returned, mid, g2, wo, wi, jnp.transpose(mlp_out))
     return jnp.transpose(out, (0, 2, 1))
 
 

time: 113 us -> 112 us (level)
  waiting for transfers between devices: 24.5 us -> 23.1 us
  Pallas kernels: 20.6 us -> 21.8 us
    all_to_all x1, waiting for transfers between devices: 24.5 us -> 23.1 us  [exchanged(): return lax.all_to_all(tiles, ROW, 0, 0, tiled=True).reshape(block.shape)]
    pallas_call x0 -> x1, Pallas kernels: none -> 1.43 us  [prep(): pl.pallas_call(prep_kernel, out_shape=(pltpu.VMEM((3 * width, width), bf1...]
  transfers between devices with their start and end apart: 1 -> 1, of which waited for: 1 -> 1; matrix products, arithmetic and copies ran while one was open for 0% -> 0% of each run, Pallas kernels for 0% -> 1%
where the time goes in v3:
time: 112 us
  blocking collectives  35.2 us (31%)
  starting transfers between devices  31 us (28%)
  waiting for transfers between devices  23.1 us (21%)
  Pallas kernels  21.8 us (19%)
    all_to_all x1, blocking collectives, exchanged(): return lax.all_to_all(tiles, ROW, 0, 0, tiled=True).reshape(block.shape)  35.2 us
    all_to_all x1, starting transfers between devices, exchanged(): return lax.all_to_all(tiles, ROW, 0, 0, tiled=True).reshape(block.shape)  31 us
    all_to_all x1, waiting for transfers between devices, exchanged(): return lax.all_to_all(tiles, ROW, 0, 0, tiled=True).reshape(block.shape)  23.1 us
    pallas_call x1, Pallas kernels, rows(): pl.pallas_call(rows_kernel, out_shape=pltpu.VMEM(got.shape, bf16), in_spe...  9.85 us
    pallas_call x1, Pallas kernels, front(): pl.pallas_call(front_kernel, out_shape=(pltpu.VMEM(cells.shape, f32), plt...  6.97 us
    pallas_call x1, Pallas kernels, tail(): pl.pallas_call(tail_kernel, out_shape=jax.ShapeDtypeStruct(mid.shape, f32...  3.51 us
  transfers between devices with their start and end apart: 1, of which 1 were waited for; matrix products, arithmetic and copies ran while one was open for 0% of the time, Pallas kernels for 1%

profile of v3, /device:TPU:33, one launch (start us, length us, event | category | flops | bytes accessed | tf_op | source)
XLA Modules:
  0.0 111.9 jit_solution(8141158501868403263)
XLA Ops:
  0.0 7.0 %front.1 = (f32[8,192,128]{2,1,0:T(8,128)S(1)}, bf16[1536,128]{1,0:T(8,128)(2,1)}) custom-call(s32[1,128]{1,0:T(1,128)} %bitcast.13, f32[8,192,128]{2,1,0:T(8,128)} %bitcast.12, f32[3,192]{1,0:T(4,128)} %gain.3, bf16[3,192,192]{2,1,0:T(8,128)(2,1)} %qkv.2, bf16[192,192]{1,0:T(8,128)(2,1)} %wout.2), custom_call_target="tpu_custom_call" | custom-call | tf_op jit(solution)/shard_map/front/pallas_call | solution.py:328
  7.0 31.0 %all-to-all-start = ((bf16[128,3,4,128]{3,2,1,0:T(4,128)(2,1)}), bf16[128,3,4,128]{3,2,1,0:T(4,128)(2,1)S(1)}, u32[]{:S(2)}, u32[]{:S(2)}) async-start(bf16[128,3,4,128]{3,2,1,0:T(4,128)(2,1)} %bitcast.2), calls=%async_computation | async-start | bytes 786432 | tf_op jit(solution)/shard_map/all_to_all | solution.py:409
  38.6 1.4 %prep.1 = (bf16[576,192]{1,0:T(8,128)(2,1)S(1)}, bf16[192,192]{1,0:T(8,128)(2,1)S(1)}, bf16[768,192]{1,0:T(8,128)(2,1)S(1)}, f32[192,256]{1,0:T(8,128)S(1)}) custom-call(f32[8,192,128]{2,1,0:T(8,128)S(1)} %get-tuple-element.12.after.mid, bf16[3,192,192]{2,1,0:T(8,128)(2,1)} %qkv.3, bf16[192,192]{1,0:T(8,128)(2,1)} %wout.3, bf16[192,768]{1,0:T(8,128)(2,1)} %w_in.1, ...), custom_call_target="tpu_custom_call" | custom-call | tf_op jit(solution)/shard_map/prep/pallas_call | solution.py:355
  40.1 23.1 %all-to-all-done = bf16[128,3,4,128]{3,2,1,0:T(4,128)(2,1)S(1)} async-done(((bf16[128,3,4,128]{3,2,1,0:T(4,128)(2,1)}), bf16[128,3,4,128]{3,2,1,0:T(4,128)(2,1)S(1)}, u32[]{:S(2)}, u32[]{:S(2)}) %all-to-all-start) | async-done | bytes 393248 | tf_op jit(solution)/shard_map/all_to_all | solution.py:409
  63.2 9.8 %rows.1 = bf16[1536,128]{1,0:T(8,128)(2,1)S(1)} custom-call(s32[1]{0:T(128)S(6)} %copy.11.n_train, bf16[1536,128]{1,0:T(8,128)(2,1)S(1)} %bitcast.8, bf16[576,192]{1,0:T(8,128)(2,1)S(1)} %get-tuple-element.13.wt), custom_call_target="tpu_custom_call" | custom-call | tf_op jit(solution)/shard_map/rows/pallas_call | solution.py:373
  73.0 0.0 copy-start
  73.0 35.2 %all_to_all.10 = bf16[128,3,4,128]{3,2,1,0:T(4,128)(2,1)S(1)} all-to-all(bf16[128,3,4,128]{3,2,1,0:T(4,128)(2,1)S(1)} %bitcast.9), channel_id=1, replica_groups=mesh['grp'=2,'row'=128] {'row'}, dimensions={0} | all-to-all | bytes 786432 | tf_op jit(solution)/shard_map/all_to_all | solution.py:409
  108.2 0.0 copy-done
  108.2 3.5 %tail.1 = f32[8,192,128]{2,1,0:T(8,128)} custom-call(bf16[1536,128]{1,0:T(8,128)(2,1)S(1)} %bitcast.10, f32[8,192,128]{2,1,0:T(8,128)S(1)} %get-tuple-element.12.after.mid, f32[192,256]{1,0:T(8,128)S(1)} %get-tuple-element.14.g2, bf16[192,192]{1,0:T(8,128)(2,1)S(1)} %get-tuple-element.15.wo, bf16[768,192]{1,0:T(8,128)(2,1)S(1)} %get-tuple-element.16.wi, ...), custom_call_target="tpu_custom_call" | custom-call | tf_op jit(solution)/shard_map/tail/pallas_call | solution.py:392
Async XLA Ops:
  7.0 56.2 %all-to-all-start = ((bf16[128,3,4,128]{3,2,1,0:T(4,128)(2,1)}), bf16[128,3,4,128]{3,2,1,0:T(4,128)(2,1)S(1)}, u32[]{:S(2)}, u32[]{:S(2)}) async-start(bf16[128,3,4,128]{3,2,1,0:T(4,128)(2,1)} %bitcast.2), calls=%async_computation | async-start | bytes 786432 | tf_op jit(solution)/shard_map/all_to_all | solution.py:409
  73.0 35.2 %copy-start = (bf16[768,192]{0,1:T(8,128)(2,1)S(1)}, bf16[768,192]{0,1:T(8,128)(2,1)}, u32[]{:S(2)}) copy-start(bf16[768,192]{0,1:T(8,128)(2,1)} %param.19) | copy-start | bytes 884740

commit v4 on v3

--- a/solution.py
+++ b/solution.py
@@ -89,7 +89,7 @@
 
 
 def front_kernel(
-    present, cells, gain, qkv, wout, mid, send, raw, wq, wo, xn, qs, ks, vs, ctx, wt, cell_sems, sems
+    present, cells, gain, qkv, wout, mid, send, raw, wq, wo, live, gains, packed, xn, qs, ks, vs, ctx, wt, cell_sems, sems, out_sems
 ):
     rows, width, feats = cells.shape
     head = width // HEADS
@@ -98,9 +98,13 @@
     copies = [pltpu.make_async_copy(cells.at[r], raw.at[r], cell_sems.at[r]) for r in range(rows)]
     first = pltpu.make_async_copy(qkv, wq, sems.at[0])
     second = pltpu.make_async_copy(wout, wo, sems.at[1])
+    third = pltpu.make_async_copy(gain, gains, sems.at[2])
+    fourth = pltpu.make_async_copy(present, live, sems.at[3])
+    third.start()
+    fourth.start()
+    first.start()
     copies[0].start()
     copies[1].start()
-    first.start()
     for c in copies[2:]:
         c.start()
     second.start()
@@ -114,18 +118,18 @@
     for h in range(HEADS):
         at = h * (head + 16) + head
         vs[at : at + 16, :] = jnp.ones((16, rows * feats), bf16)
-    g0 = jnp.broadcast_to(column(gain[0:1, :]), (width, feats))
-    g1 = jnp.broadcast_to(column(gain[1:2, :]), (width, feats))
-    bias = jnp.where(present[...] > 0, 0.0, masked_score)
+    for c in (third, fourth, first, *copies, second):
+        c.wait()
+    g0 = jnp.broadcast_to(column(gains[0:1, :]), (width, feats))
+    g1 = jnp.broadcast_to(column(gains[1:2, :]), (width, feats))
+    bias = jnp.where(live[...] > 0, 0.0, masked_score)
     bias = jnp.concatenate([bias, bias], axis=1)
     last = jnp.where(iota((head, step), 0) == 0, bias, 0.0).astype(bf16)
-    first.wait()
     prepare_weights(wq, wt)
+    wot = wo[...].T
     scale = (1.0 / math.sqrt(head)) * math.log2(math.e)
 
     def normed(c):
-        copies[2 * c].wait()
-        copies[2 * c + 1].wait()
         return jnp.concatenate([layer_norm(raw[2 * c + k], g0).astype(bf16) for k in range(2)], axis=1)
 
     def place(c, triple):
@@ -145,14 +149,6 @@
                 qs[h // 2, up + 2 * head : up + 3 * head, col : col + feats] = qh[mine, part]
             ks[tok, h * 128 : (h + 1) * 128] = jnp.concatenate([kh[mine], kh[mine], kl[mine], last], axis=0).T
 
-    xt = normed(0)
-    triple = nn(wt[...], xt)
-    for c in range(chunks):
-        if c + 1 < chunks:
-            ahead = nn(wt[...], normed(c + 1))
-        place(c, triple)
-        triple = ahead
-
     def scores(r):
         at = slice(r * feats, (r + 1) * feats)
         return [nn(ks[at, p * 256 : (p + 1) * 256], qs[p, :, r * step : (r + 1) * step]) for p in range(HEADS // 2)]
@@ -168,15 +164,6 @@
                 inverse = 1.0 / o[row + head : row + head + 1, lane]
                 ctx[h * head : (h + 1) * head, at] = (o[row : row + head, lane] * inverse).astype(bf16)
 
-    s = scores(0)
-    for r in range(rows):
-        if r + 1 < rows:
-            ahead = scores(r + 1)
-        attend(r, s)
-        s = ahead
-    second.wait()
-    wot = wo[...].T
-
     def close(c, both):
         for k in range(2):
             r = 2 * c + k
@@ -184,12 +171,20 @@
             mid[r] = m
             xn[r * feats : (r + 1) * feats, :] = layer_norm(m, g1).astype(bf16).T
 
-    both = nn(wot, ctx[:, 0:step])
-    for c in range(chunks):
-        if c + 1 < chunks:
-            ahead = nn(wot, ctx[:, (c + 1) * step : (c + 2) * step])
-        close(c, both)
-        both = ahead
+    triples, found, both = {}, {}, {}
+    for t in range(chunks + 3):
+        if t < chunks:
+            triples[t] = nn(wt[...], normed(t))
+        if 0 <= t - 2 < chunks:
+            for r in (2 * t - 4, 2 * t - 3):
+                attend(r, found.pop(r))
+            both[t - 2] = nn(wot, ctx[:, (t - 2) * step : (t - 1) * step])
+        if 0 <= t - 1 < chunks:
+            place(t - 1, triples.pop(t - 1))
+            for r in (2 * t - 2, 2 * t - 1):
+                found[r] = scores(r)
+        if 0 <= t - 3 < chunks:
+            close(t - 3, both.pop(t - 3))
     shape = (192, rows * 16)
     o, t = iota(shape, 0), iota(shape, 1)
     f, r = t & 15, t >> 4
@@ -198,12 +193,18 @@
     first_half = onehot((o == base + 8 + (r & 3)) & (r < 4))
     second_half = onehot((o == base + 8 + (r & 3)) & (r >= 4))
     lane = iota((192, 128), 1)
+    sent = []
     for b in range(feats // 16):
         x = jnp.concatenate([xn[k * feats + b * 16 : k * feats + b * 16 + 16, :] for k in range(rows)], axis=0)
         tail = x[:, 128:width]
         tails = jnp.concatenate([tail, tail], axis=1)
         out = nn(low, x[:, 0:128]) + jnp.where(lane < 64, nn(first_half, tails), nn(second_half, tails))
-        send[b * 192 : (b + 1) * 192, :] = out.astype(bf16)
+        at = slice(b * 192, (b + 1) * 192)
+        packed[at, :] = out.astype(bf16)
+        sent.append(pltpu.make_async_copy(packed.at[at, :], send.at[at, :], out_sems.at[b]))
+        sent[-1].start()
+    for c in sent:
+        c.wait()
 
 
 def prep_kernel(after, qkv, wout, w_in, gain, wt, wo, wi, g2):
@@ -236,15 +237,22 @@
         project(nt(wt[...], xn[at, :]), bias, at, qs, ks, vs, head)
 
     tiles = total // 256
-    blocks = total // 256
+    blocks = total // 512
 
     def score(h, cols, b):
-        s = nn(ks[b * 256 : (b + 1) * 256, h * 128 : (h + 1) * 128], qs[h, :, cols])
-        sbuf[h % 2, b * 256 : (b + 1) * 256, :] = s
-        return jnp.max(s.reshape(32, 8, 256), axis=0)
+        s = nn(ks[b * 512 : (b + 1) * 512, h * 128 : (h + 1) * 128], qs[h, :, cols])
+        sbuf[h % 2, b * 512 : (b + 1) * 512, :] = s
+        return jnp.max(s.reshape(512 // 8, 8, 256), axis=0)
 
     def columns(j):
         return pl.ds(pl.multiple_of(j * 256, 256), 256)
+
+    def gather(h, b, w, o):
+        part = nn(vs[h, :, b * 512 : (b + 1) * 512], w)
+        return part if o is None else o + part
+
+    def finish(h, cols, o):
+        ctx[h * head : (h + 1) * head, cols] = (o[0:head] * (1.0 / o[head : head + 1])).astype(bf16)
 
     peak = score(0, slice(0, 256), 0)
     for b in range(1, blocks):
@@ -253,17 +261,24 @@
     def query_tile(j, peak):
         cols = columns(j)
         after = columns(jnp.minimum(j + 1, tiles - 1))
+        held = []
+        o = None
         for h in range(HEADS):
             top = jnp.max(peak, axis=0, keepdims=True)
-            o = None
             peak = None
             for b in range(blocks):
                 ahead = score(h + 1, cols, b) if h + 1 < HEADS else score(0, after, b)
                 peak = ahead if peak is None else jnp.maximum(peak, ahead)
-                w = jnp.exp2(sbuf[h % 2, b * 256 : (b + 1) * 256, :] - top).astype(bf16)
-                part = nn(vs[h, :, b * 256 : (b + 1) * 256], w)
-                o = part if o is None else o + part
-            ctx[h * head : (h + 1) * head, cols] = (o[0:head] * (1.0 / o[head : head + 1])).astype(bf16)
+                held.append((h, b, jnp.exp2(sbuf[h % 2, b * 512 : (b + 1) * 512, :] - top).astype(bf16)))
+                while len(held) > 1:
+                    hh, bb, w = held.pop(0)
+                    o = gather(hh, bb, w, None if bb == 0 else o)
+                    if bb == blocks - 1:
+                        finish(hh, cols, o)
+        for hh, bb, w in held:
+            o = gather(hh, bb, w, None if bb == 0 else o)
+            if bb == blocks - 1:
+                finish(hh, cols, o)
         return peak
 
     lax.fori_loop(0, tiles, query_tile, peak)
@@ -297,17 +312,24 @@
             ctx[at, 0:128] = lo[r * 16 : (r + 1) * 16]
             ctx[at, 128:width] = hi[r * 16 : (r + 1) * 16]
     sent = []
-    for c in range(rows // 2):
-        old = jnp.concatenate([mid[2 * c], mid[2 * c + 1]], axis=1)
-        late = old + nt(wo[...], ctx[c * 2 * feats : (c + 1) * 2 * feats, :])
-        n3 = layer_norm(late, g2[...]).astype(bf16)
-        z = nn(wi[...], n3)
-        hidden = (z * 0.5 * (1.0 + lax.erf(z * math.sqrt(0.5)))).astype(bf16)
-        out = late + nn(w_out[...], hidden)
-        for k in range(2):
-            out_buf[2 * c + k] = out[:, k * feats : (k + 1) * feats]
-            sent.append(pltpu.make_async_copy(out_buf.at[2 * c + k], result.at[2 * c + k], sems.at[2 * c + k]))
-            sent[-1].start()
+    chunks = rows // 2
+    late, z, hidden = {}, {}, {}
+    for t in range(chunks + 3):
+        if t < chunks:
+            old = jnp.concatenate([mid[2 * t], mid[2 * t + 1]], axis=1)
+            late[t] = old + nt(wo[...], ctx[t * 2 * feats : (t + 1) * 2 * feats, :])
+        if 0 <= t - 2 < chunks:
+            v = z.pop(t - 2)
+            hidden[t - 2] = (v * 0.5 * (1.0 + lax.erf(v * math.sqrt(0.5)))).astype(bf16)
+        if 0 <= t - 1 < chunks:
+            z[t - 1] = nn(wi[...], layer_norm(late[t - 1], g2[...]).astype(bf16))
+        if 0 <= t - 3 < chunks:
+            c = t - 3
+            out = late.pop(c) + nn(w_out[...], hidden.pop(c))
+            for k in range(2):
+                out_buf[2 * c + k] = out[:, k * feats : (k + 1) * feats]
+                sent.append(pltpu.make_async_copy(out_buf.at[2 * c + k], result.at[2 * c + k], sems.at[2 * c + k]))
+                sent[-1].start()
     for s in sent:
         s.wait()
 
@@ -329,14 +351,17 @@
         front_kernel,
         out_shape=(
             pltpu.VMEM(cells.shape, f32),
-            pltpu.VMEM((tokens * width // 128, 128), bf16),
+            jax.ShapeDtypeStruct((tokens * width // 128, 128), bf16),
         ),
-        in_specs=[VMEM, ANY, VMEM, ANY, ANY],
-        out_specs=(VMEM, VMEM),
+        in_specs=[ANY] * 5,
+        out_specs=(VMEM, ANY),
         scratch_shapes=[
             pltpu.VMEM(cells.shape, f32),
             pltpu.VMEM(qkv.shape, bf16),
             pltpu.VMEM(wout.shape, bf16),
+            pltpu.VMEM(present.shape, jnp.int32),
+            pltpu.VMEM(gain.shape, f32),
+            pltpu.VMEM((tokens * width // 128, 128), bf16),
             pltpu.VMEM((tokens, width), bf16),
             pltpu.VMEM((HEADS // 2, 8 * head, 2 * tokens), bf16),
             pltpu.VMEM((tokens, HEADS * 128), bf16),
@@ -344,7 +369,8 @@
             pltpu.VMEM((width, tokens), bf16),
             pltpu.VMEM((3 * width, width), bf16),
             pltpu.SemaphoreType.DMA((rows,)),
-            pltpu.SemaphoreType.DMA((2,)),
+            pltpu.SemaphoreType.DMA((4,)),
+            pltpu.SemaphoreType.DMA((feats // 16,)),
         ],
         name="front",
     )(present, cells, gain, qkv, wout)

time: 112 us -> 107 us (0.955)
  Pallas kernels: 21.8 us -> 17 us
    pallas_call x1, Pallas kernels: 9.85 us -> 7.62 us  [rows(): pl.pallas_call(rows_kernel, out_shape=pltpu.VMEM(got.shape, bf16), in_spe...]
    pallas_call x1, Pallas kernels: 6.97 us -> 5.48 us  [front(): pl.pallas_call(front_kernel, out_shape=(pltpu.VMEM(cells.shape, f32), jax...]
where the time goes in v4:
time: 107 us
  blocking collectives  35.2 us (33%)
  starting transfers between devices  31 us (29%)
  waiting for transfers between devices  23.1 us (22%)
  Pallas kernels  17 us (16%)
    all_to_all x1, blocking collectives, exchanged(): return lax.all_to_all(tiles, ROW, 0, 0, tiled=True).reshape(block.shape)  35.2 us
    all_to_all x1, starting transfers between devices, exchanged(): return lax.all_to_all(tiles, ROW, 0, 0, tiled=True).reshape(block.shape)  31 us
    all_to_all x1, waiting for transfers between devices, exchanged(): return lax.all_to_all(tiles, ROW, 0, 0, tiled=True).reshape(block.shape)  23.1 us
    pallas_call x1, Pallas kernels, rows(): pl.pallas_call(rows_kernel, out_shape=pltpu.VMEM(got.shape, bf16), in_spe...  7.62 us
    pallas_call x1, Pallas kernels, front(): pl.pallas_call(front_kernel, out_shape=(pltpu.VMEM(cells.shape, f32), jax...  5.48 us
    pallas_call x1, Pallas kernels, tail(): pl.pallas_call(tail_kernel, out_shape=jax.ShapeDtypeStruct(mid.shape, f32...  2.52 us
  transfers between devices with their start and end apart: 1, of which 1 were waited for; matrix products, arithmetic and copies ran while one was open for 0% of the time, Pallas kernels for 1%

profile of v4, /device:TPU:33, one launch (start us, length us, event | category | flops | bytes accessed | tf_op | source)
XLA Modules:
  0.0 107.2 jit_solution(3124640731464009240)
XLA Ops:
  0.0 5.5 %front.1 = (f32[8,192,128]{2,1,0:T(8,128)S(1)}, bf16[1536,128]{1,0:T(8,128)(2,1)}) custom-call(s32[1,128]{1,0:T(1,128)} %bitcast.14, f32[8,192,128]{2,1,0:T(8,128)} %bitcast.12, f32[3,192]{1,0:T(4,128)} %gain.3, bf16[3,192,192]{2,1,0:T(8,128)(2,1)} %qkv.2, bf16[192,192]{1,0:T(8,128)(2,1)} %wout.2), custom_call_target="tpu_custom_call" | custom-call | tf_op jit(solution)/shard_map/front/pallas_call | solution.py:350
  5.5 31.0 %all-to-all-start = ((bf16[128,3,4,128]{3,2,1,0:T(4,128)(2,1)}), bf16[128,3,4,128]{3,2,1,0:T(4,128)(2,1)S(1)}, u32[]{:S(2)}, u32[]{:S(2)}) async-start(bf16[128,3,4,128]{3,2,1,0:T(4,128)(2,1)} %bitcast.13), calls=%async_computation | async-start | bytes 786432 | tf_op jit(solution)/shard_map/all_to_all | solution.py:435
  37.2 1.4 %prep.1 = (bf16[576,192]{1,0:T(8,128)(2,1)S(1)}, bf16[192,192]{1,0:T(8,128)(2,1)S(1)}, bf16[768,192]{1,0:T(8,128)(2,1)S(1)}, f32[192,256]{1,0:T(8,128)S(1)}) custom-call(f32[8,192,128]{2,1,0:T(8,128)S(1)} %get-tuple-element.12.after.mid, bf16[3,192,192]{2,1,0:T(8,128)(2,1)} %qkv.3, bf16[192,192]{1,0:T(8,128)(2,1)} %wout.3, bf16[192,768]{1,0:T(8,128)(2,1)} %w_in.1, ...), custom_call_target="tpu_custom_call" | custom-call | tf_op jit(solution)/shard_map/prep/pallas_call | solution.py:381
  38.6 23.1 %all-to-all-done = bf16[128,3,4,128]{3,2,1,0:T(4,128)(2,1)S(1)} async-done(((bf16[128,3,4,128]{3,2,1,0:T(4,128)(2,1)}), bf16[128,3,4,128]{3,2,1,0:T(4,128)(2,1)S(1)}, u32[]{:S(2)}, u32[]{:S(2)}) %all-to-all-start) | async-done | bytes 393248 | tf_op jit(solution)/shard_map/all_to_all | solution.py:435
  61.7 7.6 %rows.1 = bf16[1536,128]{1,0:T(8,128)(2,1)S(1)} custom-call(s32[1]{0:T(128)S(6)} %copy.11.n_train, bf16[1536,128]{1,0:T(8,128)(2,1)S(1)} %bitcast.8, bf16[576,192]{1,0:T(8,128)(2,1)S(1)} %get-tuple-element.13.wt), custom_call_target="tpu_custom_call" | custom-call | tf_op jit(solution)/shard_map/rows/pallas_call | solution.py:399
  69.3 0.0 copy-start
  69.3 35.2 %all_to_all.10 = bf16[128,3,4,128]{3,2,1,0:T(4,128)(2,1)S(1)} all-to-all(bf16[128,3,4,128]{3,2,1,0:T(4,128)(2,1)S(1)} %bitcast.9), channel_id=1, replica_groups=mesh['grp'=2,'row'=128] {'row'}, dimensions={0} | all-to-all | bytes 786432 | tf_op jit(solution)/shard_map/all_to_all | solution.py:435
  104.5 0.0 copy-done
  104.5 2.5 %tail.1 = f32[8,192,128]{2,1,0:T(8,128)} custom-call(bf16[1536,128]{1,0:T(8,128)(2,1)S(1)} %bitcast.10, f32[8,192,128]{2,1,0:T(8,128)S(1)} %get-tuple-element.12.after.mid, f32[192,256]{1,0:T(8,128)S(1)} %get-tuple-element.14.g2, bf16[192,192]{1,0:T(8,128)(2,1)S(1)} %get-tuple-element.15.wo, bf16[768,192]{1,0:T(8,128)(2,1)S(1)} %get-tuple-element.16.wi, ...), custom_call_target="tpu_custom_call" | custom-call | tf_op jit(solution)/shard_map/tail/pallas_call | solution.py:418
Async XLA Ops:
  5.5 56.2 %all-to-all-start = ((bf16[128,3,4,128]{3,2,1,0:T(4,128)(2,1)}), bf16[128,3,4,128]{3,2,1,0:T(4,128)(2,1)S(1)}, u32[]{:S(2)}, u32[]{:S(2)}) async-start(bf16[128,3,4,128]{3,2,1,0:T(4,128)(2,1)} %bitcast.13), calls=%async_computation | async-start | bytes 786432 | tf_op jit(solution)/shard_map/all_to_all | solution.py:435
  69.3 35.2 %copy-start = (bf16[768,192]{0,1:T(8,128)(2,1)S(1)}, bf16[768,192]{0,1:T(8,128)(2,1)}, u32[]{:S(2)}) copy-start(bf16[768,192]{0,1:T(8,128)(2,1)} %param.19) | copy-start | bytes 884740

commit v5 on v4

--- a/solution.py
+++ b/solution.py
@@ -86,6 +86,36 @@
         vs[h, 0:head, rows] = v[mine]
         stack = jnp.concatenate([kh[mine], kh[mine], kl[mine], last], axis=0)
         ks[rows, h * 128 : (h + 1) * 128] = stack.T
+
+
+def swapped(v):
+    return pltpu.roll(v, 4, axis=1)
+
+
+def opened(block):
+    a = block.astype(f32).reshape(-1, 24, 128)
+    upper = iota((a.shape[0], 8, 128), 1) < 4
+    v0, v1, v2 = a[:, 0:8], a[:, 8:16], a[:, 16:24]
+    v3 = swapped(jnp.where(upper, v2, v1))
+    h = jnp.where(upper, v1, v2)
+    turned = pltpu.roll(h, 64, axis=2)
+    d0 = jnp.where(upper, h, swapped(turned))
+    d1 = jnp.where(upper, swapped(h), turned)
+    low = jnp.concatenate([v0, v3], axis=1).reshape(-1, 128)
+    high = jnp.concatenate([d0, d1], axis=1).reshape(-1, 128)
+    return low.astype(bf16), high[:, 0:64].astype(bf16)
+
+
+def closed(low, twice):
+    low = low.reshape(-1, 16, 128)
+    twice = twice.reshape(-1, 16, 128)
+    shape = (low.shape[0], 8, 128)
+    upper, left = iota(shape, 1) < 4, iota(shape, 2) < 64
+    d0, d1 = twice[:, 0:8], twice[:, 8:16]
+    h = jnp.where(upper, jnp.where(left, d0, swapped(d0)), jnp.where(left, swapped(d1), d1))
+    v3 = swapped(low[:, 8:16])
+    out = jnp.concatenate([low[:, 0:8], jnp.where(upper, h, v3), jnp.where(upper, v3, h)], axis=1)
+    return out.reshape(-1, 128).astype(bf16)
 
 
 def front_kernel(
@@ -185,22 +215,16 @@
                 found[r] = scores(r)
         if 0 <= t - 3 < chunks:
             close(t - 3, both.pop(t - 3))
-    shape = (192, rows * 16)
-    o, t = iota(shape, 0), iota(shape, 1)
-    f, r = t & 15, t >> 4
-    base = f * 12
-    low = onehot(o == base + r)
-    first_half = onehot((o == base + 8 + (r & 3)) & (r < 4))
-    second_half = onehot((o == base + 8 + (r & 3)) & (r >= 4))
-    lane = iota((192, 128), 1)
+    shape = (16 * rows, 16 * rows)
+    to, of = iota(shape, 0), iota(shape, 1)
+    order = onehot(of == (to % rows) * 16 + to // rows)
     sent = []
     for b in range(feats // 16):
         x = jnp.concatenate([xn[k * feats + b * 16 : k * feats + b * 16 + 16, :] for k in range(rows)], axis=0)
-        tail = x[:, 128:width]
-        tails = jnp.concatenate([tail, tail], axis=1)
-        out = nn(low, x[:, 0:128]) + jnp.where(lane < 64, nn(first_half, tails), nn(second_half, tails))
+        moved = nn(order, jnp.concatenate([x, x[:, 128:width]], axis=1))
+        out = closed(moved[:, 0:128], moved[:, 128:256])
         at = slice(b * 192, (b + 1) * 192)
-        packed[at, :] = out.astype(bf16)
+        packed[at, :] = out
         sent.append(pltpu.make_async_copy(packed.at[at, :], send.at[at, :], out_sems.at[b]))
         sent[-1].start()
     for c in sent:
@@ -220,22 +244,23 @@
     head = width // HEADS
     total = xn.shape[0]
     fill_constant_rows(qs, vs, head)
-    t, p = iota((128, 192), 0), iota((128, 192), 1)
-    low = onehot(p == (t >> 3) * 12 + (t & 7))
-    high = onehot(p == (t >> 3) * 12 + 8 + (t & 3))
-    early = (iota((128, 64), 0) & 7) < 4
-    for b in range(total // 128):
-        a = got[b * 192 : (b + 1) * 192, :]
-        hi = nn(high, a)
-        xn[b * 128 : (b + 1) * 128, 0:128] = nn(low, a).astype(bf16)
-        xn[b * 128 : (b + 1) * 128, 128:width] = jnp.where(early, hi[:, 0:64], hi[:, 64:128]).astype(bf16)
     live = n_train[0]
     step = 256
+
+    def arrived(c):
+        for b in (2 * c, 2 * c + 1):
+            lo, hi = opened(got[b * 192 : (b + 1) * 192, :])
+            xn[b * 128 : (b + 1) * 128, 0:128] = lo
+            xn[b * 128 : (b + 1) * 128, 128:width] = hi
+        return nt(wt[...], xn[c * step : (c + 1) * step, :])
+
+    triple = arrived(0)
     for c in range(total // step):
-        at = slice(c * step, (c + 1) * step)
+        if c + 1 < total // step:
+            ahead = arrived(c + 1)
         bias = jnp.where(iota((1, step), 1) + c * step < live, 0.0, masked_score)
-        project(nt(wt[...], xn[at, :]), bias, at, qs, ks, vs, head)
-
+        project(triple, bias, slice(c * step, (c + 1) * step), qs, ks, vs, head)
+        triple = ahead
     tiles = total // 256
     blocks = total // 512
 
@@ -282,35 +307,24 @@
         return peak
 
     lax.fori_loop(0, tiles, query_tile, peak)
-    o, q = iota((192, 128), 0), iota((192, 128), 1)
-    base, r = (q >> 3) * 12, q & 7
-    low = onehot(o == base + r)
-    first = onehot((o == base + 8 + (r & 3)) & (r < 4))
-    second = onehot((o == base + 8 + (r & 3)) & (r >= 4))
-    lane = iota((192, 128), 1)
     for b in range(total // 128):
         at = slice(b * 128, (b + 1) * 128)
-        tail = ctx[128:width, at]
-        tails = jnp.concatenate([tail, tail], axis=0)
-        out = nt(low, ctx[0:128, at]) + jnp.where(lane < 64, nt(first, tails), nt(second, tails))
-        send[b * 192 : (b + 1) * 192, :] = out.astype(bf16)
+        end = ctx[128:width, at]
+        twice = jnp.concatenate([end, end], axis=0).T
+        send[b * 192 : (b + 1) * 192, :] = closed(ctx[0:128, at].T.astype(f32), twice.astype(f32))
 
 
 def tail_kernel(got, mid, g2, wo, wi, w_out, result, ctx, out_buf, sems):
     rows, width, feats = mid.shape
-    t, p = iota((128, 192), 0), iota((128, 192), 1)
-    low = onehot(p == (t & 15) * 12 + (t >> 4))
-    high = onehot(p == (t & 15) * 12 + 8 + ((t >> 4) & 3))
-    early = iota((128, 64), 0) < 64
+    shape = (16 * rows, 16 * rows)
+    to, of = iota(shape, 0), iota(shape, 1)
+    order = onehot(of == (to % 16) * rows + to // 16)
     for b in range(feats // 16):
-        a = got[b * 192 : (b + 1) * 192, :]
-        hi = nn(high, a)
-        lo = nn(low, a).astype(bf16)
-        hi = jnp.where(early, hi[:, 0:64], hi[:, 64:128]).astype(bf16)
+        lo, hi = opened(got[b * 192 : (b + 1) * 192, :])
+        x = nn(order, jnp.concatenate([lo, hi], axis=1)).astype(bf16)
         for r in range(rows):
             at = slice(r * feats + b * 16, r * feats + b * 16 + 16)
-            ctx[at, 0:128] = lo[r * 16 : (r + 1) * 16]
-            ctx[at, 128:width] = hi[r * 16 : (r + 1) * 16]
+            ctx[at, :] = x[r * 16 : (r + 1) * 16]
     sent = []
     chunks = rows // 2
     late, z, hidden = {}, {}, {}

time: 107 us -> 107 us (level)
  no operation moved by 1% of the time
where the time goes in v5:
time: 107 us; the launch traced here: 106 us
  blocking collectives  35.2 us (33%)
  starting transfers between devices  31 us (29%)
  waiting for transfers between devices  23.1 us (22%)
  Pallas kernels  16.1 us (15%)
    all_to_all x1, blocking collectives, exchanged(): return lax.all_to_all(tiles, ROW, 0, 0, tiled=True).reshape(block.shape)  35.2 us
    all_to_all x1, starting transfers between devices, exchanged(): return lax.all_to_all(tiles, ROW, 0, 0, tiled=True).reshape(block.shape)  31 us
    all_to_all x1, waiting for transfers between devices, exchanged(): return lax.all_to_all(tiles, ROW, 0, 0, tiled=True).reshape(block.shape)  23.1 us
    pallas_call x1, Pallas kernels, rows(): pl.pallas_call(rows_kernel, out_shape=pltpu.VMEM(got.shape, bf16), in_spe...  6.92 us
    pallas_call x1, Pallas kernels, front(): pl.pallas_call(front_kernel, out_shape=(pltpu.VMEM(cells.shape, f32), jax...  5.29 us
    pallas_call x1, Pallas kernels, tail(): pl.pallas_call(tail_kernel, out_shape=jax.ShapeDtypeStruct(mid.shape, f32...  2.46 us
  transfers between devices with their start and end apart: 1, of which 1 were waited for; matrix products, arithmetic and copies ran while one was open for 0% of the time, Pallas kernels for 1%

profile of v5, /device:TPU:33, one launch (start us, length us, event | category | flops | bytes accessed | tf_op | source)
XLA Modules:
  0.0 106.2 jit_solution(6342864993170917118)
XLA Ops:
  0.0 5.3 %front.1 = (f32[8,192,128]{2,1,0:T(8,128)S(1)}, bf16[1536,128]{1,0:T(8,128)(2,1)}) custom-call(s32[1,128]{1,0:T(1,128)} %bitcast.14, f32[8,192,128]{2,1,0:T(8,128)} %bitcast.12, f32[3,192]{1,0:T(4,128)} %gain.3, bf16[3,192,192]{2,1,0:T(8,128)(2,1)} %qkv.2, bf16[192,192]{1,0:T(8,128)(2,1)} %wout.2), custom_call_target="tpu_custom_call" | custom-call | tf_op jit(solution)/shard_map/front/pallas_call | solution.py:364
  5.3 31.0 %all-to-all-start = ((bf16[128,3,4,128]{3,2,1,0:T(4,128)(2,1)}), bf16[128,3,4,128]{3,2,1,0:T(4,128)(2,1)S(1)}, u32[]{:S(2)}, u32[]{:S(2)}) async-start(bf16[128,3,4,128]{3,2,1,0:T(4,128)(2,1)} %bitcast.13), calls=%async_computation | async-start | bytes 786432 | tf_op jit(solution)/shard_map/all_to_all | solution.py:449
  37.0 1.4 %prep.1 = (bf16[576,192]{1,0:T(8,128)(2,1)S(1)}, bf16[192,192]{1,0:T(8,128)(2,1)S(1)}, bf16[768,192]{1,0:T(8,128)(2,1)S(1)}, f32[192,256]{1,0:T(8,128)S(1)}) custom-call(f32[8,192,128]{2,1,0:T(8,128)S(1)} %get-tuple-element.12.after.mid, bf16[3,192,192]{2,1,0:T(8,128)(2,1)} %qkv.3, bf16[192,192]{1,0:T(8,128)(2,1)} %wout.3, bf16[192,768]{1,0:T(8,128)(2,1)} %w_in.1, ...), custom_call_target="tpu_custom_call" | custom-call | tf_op jit(solution)/shard_map/prep/pallas_call | solution.py:395
  38.4 23.1 %all-to-all-done = bf16[128,3,4,128]{3,2,1,0:T(4,128)(2,1)S(1)} async-done(((bf16[128,3,4,128]{3,2,1,0:T(4,128)(2,1)}), bf16[128,3,4,128]{3,2,1,0:T(4,128)(2,1)S(1)}, u32[]{:S(2)}, u32[]{:S(2)}) %all-to-all-start) | async-done | bytes 393248 | tf_op jit(solution)/shard_map/all_to_all | solution.py:449
  61.5 6.9 %rows.1 = bf16[1536,128]{1,0:T(8,128)(2,1)S(1)} custom-call(s32[1]{0:T(128)S(6)} %copy.11.n_train, bf16[1536,128]{1,0:T(8,128)(2,1)S(1)} %bitcast.8, bf16[576,192]{1,0:T(8,128)(2,1)S(1)} %get-tuple-element.13.wt), custom_call_target="tpu_custom_call" | custom-call | tf_op jit(solution)/shard_map/rows/pallas_call | solution.py:413
  68.4 0.0 copy-start
  68.4 35.2 %all_to_all.10 = bf16[128,3,4,128]{3,2,1,0:T(4,128)(2,1)S(1)} all-to-all(bf16[128,3,4,128]{3,2,1,0:T(4,128)(2,1)S(1)} %bitcast.9), channel_id=1, replica_groups=mesh['grp'=2,'row'=128] {'row'}, dimensions={0} | all-to-all | bytes 786432 | tf_op jit(solution)/shard_map/all_to_all | solution.py:449
  103.6 0.0 copy-done
  103.6 2.5 %tail.1 = f32[8,192,128]{2,1,0:T(8,128)} custom-call(bf16[1536,128]{1,0:T(8,128)(2,1)S(1)} %bitcast.10, f32[8,192,128]{2,1,0:T(8,128)S(1)} %get-tuple-element.12.after.mid, f32[192,256]{1,0:T(8,128)S(1)} %get-tuple-element.14.g2, bf16[192,192]{1,0:T(8,128)(2,1)S(1)} %get-tuple-element.15.wo, bf16[768,192]{1,0:T(8,128)(2,1)S(1)} %get-tuple-element.16.wi, ...), custom_call_target="tpu_custom_call" | custom-call | tf_op jit(solution)/shard_map/tail/pallas_call | solution.py:432
Async XLA Ops:
  5.3 56.2 %all-to-all-start = ((bf16[128,3,4,128]{3,2,1,0:T(4,128)(2,1)}), bf16[128,3,4,128]{3,2,1,0:T(4,128)(2,1)S(1)}, u32[]{:S(2)}, u32[]{:S(2)}) async-start(bf16[128,3,4,128]{3,2,1,0:T(4,128)(2,1)} %bitcast.13), calls=%async_computation | async-start | bytes 786432 | tf_op jit(solution)/shard_map/all_to_all | solution.py:449
  68.4 35.2 %copy-start = (bf16[768,192]{0,1:T(8,128)(2,1)S(1)}, bf16[768,192]{0,1:T(8,128)(2,1)}, u32[]{:S(2)}) copy-start(bf16[768,192]{0,1:T(8,128)(2,1)} %param.19) | copy-start | bytes 884740

commit v6 on v5

--- a/solution.py
+++ b/solution.py
@@ -1,3 +1,4 @@
+import functools
 import math
 
 import jax
@@ -262,51 +263,60 @@
         project(triple, bias, slice(c * step, (c + 1) * step), qs, ks, vs, head)
         triple = ahead
     tiles = total // 256
-    blocks = total // 512
-
-    def score(h, cols, b):
-        s = nn(ks[b * 512 : (b + 1) * 512, h * 128 : (h + 1) * 128], qs[h, :, cols])
-        sbuf[h % 2, b * 512 : (b + 1) * 512, :] = s
-        return jnp.max(s.reshape(512 // 8, 8, 256), axis=0)
+    deep = sbuf.shape[0]
 
     def columns(j):
         return pl.ds(pl.multiple_of(j * 256, 256), 256)
 
+    def score(h, cols, b):
+        s = nn(ks[b * 256 : (b + 1) * 256, h * 128 : (h + 1) * 128], qs[h, :, cols])
+        sbuf[h % deep, b * 256 : (b + 1) * 256, :] = s
+        return jnp.max(s.reshape(32, 8, 256), axis=0)
+
     def gather(h, b, w, o):
-        part = nn(vs[h, :, b * 512 : (b + 1) * 512], w)
+        part = nn(vs[h, :, b * 256 : (b + 1) * 256], w)
         return part if o is None else o + part
 
     def finish(h, cols, o):
         ctx[h * head : (h + 1) * head, cols] = (o[0:head] * (1.0 / o[head : head + 1])).astype(bf16)
 
-    peak = score(0, slice(0, 256), 0)
-    for b in range(1, blocks):
-        peak = jnp.maximum(peak, score(0, slice(0, 256), b))
-
-    def query_tile(j, peak):
-        cols = columns(j)
-        after = columns(jnp.minimum(j + 1, tiles - 1))
-        held = []
-        o = None
-        for h in range(HEADS):
-            top = jnp.max(peak, axis=0, keepdims=True)
-            peak = None
-            for b in range(blocks):
-                ahead = score(h + 1, cols, b) if h + 1 < HEADS else score(0, after, b)
-                peak = ahead if peak is None else jnp.maximum(peak, ahead)
-                held.append((h, b, jnp.exp2(sbuf[h % 2, b * 512 : (b + 1) * 512, :] - top).astype(bf16)))
-                while len(held) > 1:
-                    hh, bb, w = held.pop(0)
-                    o = gather(hh, bb, w, None if bb == 0 else o)
-                    if bb == blocks - 1:
-                        finish(hh, cols, o)
-        for hh, bb, w in held:
-            o = gather(hh, bb, w, None if bb == 0 else o)
-            if bb == blocks - 1:
-                finish(hh, cols, o)
-        return peak
-
-    lax.fori_loop(0, tiles, query_tile, peak)
+    def attend(blocks):
+        peaks = []
+        for h in range(deep - 1):
+            found = [score(h, slice(0, 256), b) for b in range(blocks)]
+            peaks.append(functools.reduce(jnp.maximum, found))
+
+        def query_tile(j, peaks):
+            cols = columns(j)
+            after = columns(jnp.minimum(j + 1, tiles - 1))
+            held = []
+            o = None
+            peaks = list(peaks)
+
+            def settle(o):
+                h, b, w = held.pop(0)
+                o = gather(h, b, w, None if b == 0 else o)
+                if b == blocks - 1:
+                    finish(h, cols, o)
+                return o
+
+            for h in range(HEADS):
+                top = jnp.max(peaks.pop(0), axis=0, keepdims=True)
+                n = h + deep - 1
+                found = []
+                for b in range(blocks):
+                    found.append(score(n % HEADS, cols if n < HEADS else after, b))
+                    held.append((h, b, jnp.exp2(sbuf[h % deep, b * 256 : (b + 1) * 256, :] - top).astype(bf16)))
+                    if len(held) > 1:
+                        o = settle(o)
+                peaks.append(functools.reduce(jnp.maximum, found))
+            settle(o)
+            return tuple(peaks)
+
+        lax.fori_loop(0, tiles, query_tile, tuple(peaks), unroll=2)
+
+    for blocks in range(1, total // 256 + 1):
+        pl.when((live + 255) // 256 == blocks)(functools.partial(attend, blocks))
     for b in range(total // 128):
         at = slice(b * 128, (b + 1) * 128)
         end = ctx[128:width, at]
@@ -421,7 +431,7 @@
             pltpu.VMEM((tokens, HEADS * 128), bf16),
             pltpu.VMEM((HEADS, head + 16, tokens), bf16),
             pltpu.VMEM((width, tokens), bf16),
-            pltpu.VMEM((2, tokens, 256), f32),
+            pltpu.VMEM((3, tokens, 256), f32),
         ],
         name="rows",
     )(n_train, near(got), near(wt))

time: 107 us -> 105 us (0.981)
  Pallas kernels: 16.1 us -> 14.8 us
    pallas_call x1, Pallas kernels: 6.92 us -> 5.62 us  [rows(): pl.pallas_call(rows_kernel, out_shape=pltpu.VMEM(got.shape, bf16), in_spe...]
where the time goes in v6:
time: 105 us
  blocking collectives  35.2 us (34%)
  starting transfers between devices  31 us (30%)
  waiting for transfers between devices  23.1 us (22%)
  Pallas kernels  14.8 us (14%)
    all_to_all x1, blocking collectives, exchanged(): return lax.all_to_all(tiles, ROW, 0, 0, tiled=True).reshape(block.shape)  35.2 us
    all_to_all x1, starting transfers between devices, exchanged(): return lax.all_to_all(tiles, ROW, 0, 0, tiled=True).reshape(block.shape)  31 us
    all_to_all x1, waiting for transfers between devices, exchanged(): return lax.all_to_all(tiles, ROW, 0, 0, tiled=True).reshape(block.shape)  23.1 us
    pallas_call x1, Pallas kernels, rows(): pl.pallas_call(rows_kernel, out_shape=pltpu.VMEM(got.shape, bf16), in_spe...  5.62 us
    pallas_call x1, Pallas kernels, front(): pl.pallas_call(front_kernel, out_shape=(pltpu.VMEM(cells.shape, f32), jax...  5.29 us
    pallas_call x1, Pallas kernels, tail(): pl.pallas_call(tail_kernel, out_shape=jax.ShapeDtypeStruct(mid.shape, f32...  2.46 us
  transfers between devices with their start and end apart: 1, of which 1 were waited for; matrix products, arithmetic and copies ran while one was open for 0% of the time, Pallas kernels for 1%

profile of v6, /device:TPU:33, one launch (start us, length us, event | category | flops | bytes accessed | tf_op | source)
XLA Modules:
  0.0 105.0 jit_solution(4666633449241721357)
XLA Ops:
  0.0 5.3 %front.1 = (f32[8,192,128]{2,1,0:T(8,128)S(1)}, bf16[1536,128]{1,0:T(8,128)(2,1)}) custom-call(s32[1,128]{1,0:T(1,128)} %bitcast.14, f32[8,192,128]{2,1,0:T(8,128)} %bitcast.12, f32[3,192]{1,0:T(4,128)} %gain.3, bf16[3,192,192]{2,1,0:T(8,128)(2,1)} %qkv.2, bf16[192,192]{1,0:T(8,128)(2,1)} %wout.2), custom_call_target="tpu_custom_call" | custom-call | tf_op jit(solution)/shard_map/front/pallas_call | solution.py:374
  5.3 31.0 %all-to-all-start = ((bf16[128,3,4,128]{3,2,1,0:T(4,128)(2,1)}), bf16[128,3,4,128]{3,2,1,0:T(4,128)(2,1)S(1)}, u32[]{:S(2)}, u32[]{:S(2)}) async-start(bf16[128,3,4,128]{3,2,1,0:T(4,128)(2,1)} %bitcast.13), calls=%async_computation | async-start | bytes 786432 | tf_op jit(solution)/shard_map/all_to_all | solution.py:459
  37.0 1.4 %prep.1 = (bf16[576,192]{1,0:T(8,128)(2,1)S(1)}, bf16[192,192]{1,0:T(8,128)(2,1)S(1)}, bf16[768,192]{1,0:T(8,128)(2,1)S(1)}, f32[192,256]{1,0:T(8,128)S(1)}) custom-call(f32[8,192,128]{2,1,0:T(8,128)S(1)} %get-tuple-element.12.after.mid, bf16[3,192,192]{2,1,0:T(8,128)(2,1)} %qkv.3, bf16[192,192]{1,0:T(8,128)(2,1)} %wout.3, bf16[192,768]{1,0:T(8,128)(2,1)} %w_in.1, ...), custom_call_target="tpu_custom_call" | custom-call | tf_op jit(solution)/shard_map/prep/pallas_call | solution.py:405
  38.4 23.1 %all-to-all-done = bf16[128,3,4,128]{3,2,1,0:T(4,128)(2,1)S(1)} async-done(((bf16[128,3,4,128]{3,2,1,0:T(4,128)(2,1)}), bf16[128,3,4,128]{3,2,1,0:T(4,128)(2,1)S(1)}, u32[]{:S(2)}, u32[]{:S(2)}) %all-to-all-start) | async-done | bytes 393248 | tf_op jit(solution)/shard_map/all_to_all | solution.py:459
  61.5 5.6 %rows.1 = bf16[1536,128]{1,0:T(8,128)(2,1)S(1)} custom-call(s32[1]{0:T(128)S(6)} %copy.11.n_train, bf16[1536,128]{1,0:T(8,128)(2,1)S(1)} %bitcast.8, bf16[576,192]{1,0:T(8,128)(2,1)S(1)} %get-tuple-element.13.wt), custom_call_target="tpu_custom_call" | custom-call | tf_op jit(solution)/shard_map/rows/pallas_call | solution.py:423
  67.1 0.0 copy-start
  67.1 35.2 %all_to_all.10 = bf16[128,3,4,128]{3,2,1,0:T(4,128)(2,1)S(1)} all-to-all(bf16[128,3,4,128]{3,2,1,0:T(4,128)(2,1)S(1)} %bitcast.9), channel_id=1, replica_groups=mesh['grp'=2,'row'=128] {'row'}, dimensions={0} | all-to-all | bytes 786432 | tf_op jit(solution)/shard_map/all_to_all | solution.py:459
  102.3 0.0 copy-done
  102.3 2.5 %tail.1 = f32[8,192,128]{2,1,0:T(8,128)} custom-call(bf16[1536,128]{1,0:T(8,128)(2,1)S(1)} %bitcast.10, f32[8,192,128]{2,1,0:T(8,128)S(1)} %get-tuple-element.12.after.mid, f32[192,256]{1,0:T(8,128)S(1)} %get-tuple-element.14.g2, bf16[192,192]{1,0:T(8,128)(2,1)S(1)} %get-tuple-element.15.wo, bf16[768,192]{1,0:T(8,128)(2,1)S(1)} %get-tuple-element.16.wi, ...), custom_call_target="tpu_custom_call" | custom-call | tf_op jit(solution)/shard_map/tail/pallas_call | solution.py:442
Async XLA Ops:
  5.3 56.2 %all-to-all-start = ((bf16[128,3,4,128]{3,2,1,0:T(4,128)(2,1)}), bf16[128,3,4,128]{3,2,1,0:T(4,128)(2,1)S(1)}, u32[]{:S(2)}, u32[]{:S(2)}) async-start(bf16[128,3,4,128]{3,2,1,0:T(4,128)(2,1)} %bitcast.13), calls=%async_computation | async-start | bytes 786432 | tf_op jit(solution)/shard_map/all_to_all | solution.py:459
  67.1 35.2 %copy-start = (bf16[768,192]{0,1:T(8,128)(2,1)S(1)}, bf16[768,192]{0,1:T(8,128)(2,1)}, u32[]{:S(2)}) copy-start(bf16[768,192]{0,1:T(8,128)(2,1)} %param.19) | copy-start | bytes 884740

commit v7 on v6

--- a/solution.py
+++ b/solution.py
@@ -255,23 +255,31 @@
             xn[b * 128 : (b + 1) * 128, 128:width] = hi
         return nt(wt[...], xn[c * step : (c + 1) * step, :])
 
+    tiles = total // 256
+    deep = sbuf.shape[0]
+
+    def columns(j):
+        return pl.ds(pl.multiple_of(j * 256, 256), 256)
+
+    def score(h, cols, b):
+        s = nn(ks[b * 256 : (b + 1) * 256, h * 128 : (h + 1) * 128], qs[h, :, cols])
+        sbuf[h % deep, b * 256 : (b + 1) * 256, :] = s
+        return jnp.max(s.reshape(32, 8, 256), axis=0)
+
     triple = arrived(0)
+    opening = [[] for _ in range(deep - 1)]
     for c in range(total // step):
         if c + 1 < total // step:
             ahead = arrived(c + 1)
         bias = jnp.where(iota((1, step), 1) + c * step < live, 0.0, masked_score)
         project(triple, bias, slice(c * step, (c + 1) * step), qs, ks, vs, head)
+        if c > 0:
+            for h in range(deep - 1):
+                opening[h].append(score(h, slice(0, 256), c - 1))
         triple = ahead
-    tiles = total // 256
-    deep = sbuf.shape[0]
-
-    def columns(j):
-        return pl.ds(pl.multiple_of(j * 256, 256), 256)
-
-    def score(h, cols, b):
-        s = nn(ks[b * 256 : (b + 1) * 256, h * 128 : (h + 1) * 128], qs[h, :, cols])
-        sbuf[h % deep, b * 256 : (b + 1) * 256, :] = s
-        return jnp.max(s.reshape(32, 8, 256), axis=0)
+    for h in range(deep - 1):
+        opening[h].append(score(h, slice(0, 256), total // step - 1))
+    opening = [functools.reduce(jnp.maximum, found) for found in opening]
 
     def gather(h, b, w, o):
         part = nn(vs[h, :, b * 256 : (b + 1) * 256], w)
@@ -281,11 +289,6 @@
         ctx[h * head : (h + 1) * head, cols] = (o[0:head] * (1.0 / o[head : head + 1])).astype(bf16)
 
     def attend(blocks):
-        peaks = []
-        for h in range(deep - 1):
-            found = [score(h, slice(0, 256), b) for b in range(blocks)]
-            peaks.append(functools.reduce(jnp.maximum, found))
-
         def query_tile(j, peaks):
             cols = columns(j)
             after = columns(jnp.minimum(j + 1, tiles - 1))
@@ -313,7 +316,7 @@
             settle(o)
             return tuple(peaks)
 
-        lax.fori_loop(0, tiles, query_tile, tuple(peaks), unroll=2)
+        lax.fori_loop(0, tiles, query_tile, tuple(opening), unroll=2)
 
     for blocks in range(1, total // 256 + 1):
         pl.when((live + 255) // 256 == blocks)(functools.partial(attend, blocks))

time: 105 us -> 104 us (level); the launches traced: 105 us -> 103 us
  Pallas kernels: 14.8 us -> 12.7 us
    pallas_call x1, Pallas kernels: 5.62 us -> 3.53 us  [rows(): pl.pallas_call(rows_kernel, out_shape=pltpu.VMEM(got.shape, bf16), in_spe...]
where the time goes in v7:
time: 104 us; the launch traced here: 103 us
  blocking collectives  35.2 us (34%)
  starting transfers between devices  31 us (30%)
  waiting for transfers between devices  23.1 us (22%)
  Pallas kernels  12.7 us (12%)
    all_to_all x1, blocking collectives, exchanged(): return lax.all_to_all(tiles, ROW, 0, 0, tiled=True).reshape(block.shape)  35.2 us
    all_to_all x1, starting transfers between devices, exchanged(): return lax.all_to_all(tiles, ROW, 0, 0, tiled=True).reshape(block.shape)  31 us
    all_to_all x1, waiting for transfers between devices, exchanged(): return lax.all_to_all(tiles, ROW, 0, 0, tiled=True).reshape(block.shape)  23.1 us
    pallas_call x1, Pallas kernels, front(): pl.pallas_call(front_kernel, out_shape=(pltpu.VMEM(cells.shape, f32), jax...  5.29 us
    pallas_call x1, Pallas kernels, rows(): pl.pallas_call(rows_kernel, out_shape=pltpu.VMEM(got.shape, bf16), in_spe...  3.53 us
    pallas_call x1, Pallas kernels, tail(): pl.pallas_call(tail_kernel, out_shape=jax.ShapeDtypeStruct(mid.shape, f32...  2.47 us
  transfers between devices with their start and end apart: 1, of which 1 were waited for; matrix products, arithmetic and copies ran while one was open for 0% of the time, Pallas kernels for 1%

profile of v7, /device:TPU:33, one launch (start us, length us, event | category | flops | bytes accessed | tf_op | source)
XLA Modules:
  0.0 102.9 jit_solution(8887515821927192839)
XLA Ops:
  0.0 5.3 %front.1 = (f32[8,192,128]{2,1,0:T(8,128)S(1)}, bf16[1536,128]{1,0:T(8,128)(2,1)}) custom-call(s32[1,128]{1,0:T(1,128)} %bitcast.14, f32[8,192,128]{2,1,0:T(8,128)} %bitcast.12, f32[3,192]{1,0:T(4,128)} %gain.3, bf16[3,192,192]{2,1,0:T(8,128)(2,1)} %qkv.2, bf16[192,192]{1,0:T(8,128)(2,1)} %wout.2), custom_call_target="tpu_custom_call" | custom-call | tf_op jit(solution)/shard_map/front/pallas_call | solution.py:377
  5.3 31.0 %all-to-all-start = ((bf16[128,3,4,128]{3,2,1,0:T(4,128)(2,1)}), bf16[128,3,4,128]{3,2,1,0:T(4,128)(2,1)S(1)}, u32[]{:S(2)}, u32[]{:S(2)}) async-start(bf16[128,3,4,128]{3,2,1,0:T(4,128)(2,1)} %bitcast.13), calls=%async_computation | async-start | bytes 786432 | tf_op jit(solution)/shard_map/all_to_all | solution.py:462
  37.0 1.4 %prep.1 = (bf16[576,192]{1,0:T(8,128)(2,1)S(1)}, bf16[192,192]{1,0:T(8,128)(2,1)S(1)}, bf16[768,192]{1,0:T(8,128)(2,1)S(1)}, f32[192,256]{1,0:T(8,128)S(1)}) custom-call(f32[8,192,128]{2,1,0:T(8,128)S(1)} %get-tuple-element.12.after.mid, bf16[3,192,192]{2,1,0:T(8,128)(2,1)} %qkv.3, bf16[192,192]{1,0:T(8,128)(2,1)} %wout.3, bf16[192,768]{1,0:T(8,128)(2,1)} %w_in.1, ...), custom_call_target="tpu_custom_call" | custom-call | tf_op jit(solution)/shard_map/prep/pallas_call | solution.py:408
  38.4 23.1 %all-to-all-done = bf16[128,3,4,128]{3,2,1,0:T(4,128)(2,1)S(1)} async-done(((bf16[128,3,4,128]{3,2,1,0:T(4,128)(2,1)}), bf16[128,3,4,128]{3,2,1,0:T(4,128)(2,1)S(1)}, u32[]{:S(2)}, u32[]{:S(2)}) %all-to-all-start) | async-done | bytes 393248 | tf_op jit(solution)/shard_map/all_to_all | solution.py:462
  61.5 3.5 %rows.1 = bf16[1536,128]{1,0:T(8,128)(2,1)S(1)} custom-call(s32[1]{0:T(128)S(6)} %copy.11.n_train, bf16[1536,128]{1,0:T(8,128)(2,1)S(1)} %bitcast.8, bf16[576,192]{1,0:T(8,128)(2,1)S(1)} %get-tuple-element.13.wt), custom_call_target="tpu_custom_call" | custom-call | tf_op jit(solution)/shard_map/rows/pallas_call | solution.py:426
  65.0 0.0 copy-start
  65.1 35.2 %all_to_all.10 = bf16[128,3,4,128]{3,2,1,0:T(4,128)(2,1)S(1)} all-to-all(bf16[128,3,4,128]{3,2,1,0:T(4,128)(2,1)S(1)} %bitcast.9), channel_id=1, replica_groups=mesh['grp'=2,'row'=128] {'row'}, dimensions={0} | all-to-all | bytes 786432 | tf_op jit(solution)/shard_map/all_to_all | solution.py:462
  100.3 0.0 copy-done
  100.3 2.5 %tail.1 = f32[8,192,128]{2,1,0:T(8,128)} custom-call(bf16[1536,128]{1,0:T(8,128)(2,1)S(1)} %bitcast.10, f32[8,192,128]{2,1,0:T(8,128)S(1)} %get-tuple-element.12.after.mid, f32[192,256]{1,0:T(8,128)S(1)} %get-tuple-element.14.g2, bf16[192,192]{1,0:T(8,128)(2,1)S(1)} %get-tuple-element.15.wo, bf16[768,192]{1,0:T(8,128)(2,1)S(1)} %get-tuple-element.16.wi, ...), custom_call_target="tpu_custom_call" | custom-call | tf_op jit(solution)/shard_map/tail/pallas_call | solution.py:445
Async XLA Ops:
  5.3 56.2 %all-to-all-start = ((bf16[128,3,4,128]{3,2,1,0:T(4,128)(2,1)}), bf16[128,3,4,128]{3,2,1,0:T(4,128)(2,1)S(1)}, u32[]{:S(2)}, u32[]{:S(2)}) async-start(bf16[128,3,4,128]{3,2,1,0:T(4,128)(2,1)} %bitcast.13), calls=%async_computation | async-start | bytes 786432 | tf_op jit(solution)/shard_map/all_to_all | solution.py:462
  65.0 35.2 %copy-start = (bf16[768,192]{0,1:T(8,128)(2,1)S(1)}, bf16[768,192]{0,1:T(8,128)(2,1)}, u32[]{:S(2)}) copy-start(bf16[768,192]{0,1:T(8,128)(2,1)} %param.19) | copy-start | bytes 884740

commit v8 on v7

--- a/solution.py
+++ b/solution.py
@@ -120,7 +120,7 @@
 
 
 def front_kernel(
-    present, cells, gain, qkv, wout, mid, send, raw, wq, wo, live, gains, packed, xn, qs, ks, vs, ctx, wt, cell_sems, sems, out_sems
+    present, cells, gain, qkv, wout, n_train, mid, send, g2, count, raw, wq, wo, live, gains, xn, qs, ks, vs, ctx, wt, number, cell_sems, sems
 ):
     rows, width, feats = cells.shape
     head = width // HEADS
@@ -131,8 +131,10 @@
     second = pltpu.make_async_copy(wout, wo, sems.at[1])
     third = pltpu.make_async_copy(gain, gains, sems.at[2])
     fourth = pltpu.make_async_copy(present, live, sems.at[3])
+    fifth = pltpu.make_async_copy(n_train, number, sems.at[4])
     third.start()
     fourth.start()
+    fifth.start()
     first.start()
     copies[0].start()
     copies[1].start()
@@ -149,10 +151,12 @@
     for h in range(HEADS):
         at = h * (head + 16) + head
         vs[at : at + 16, :] = jnp.ones((16, rows * feats), bf16)
-    for c in (third, fourth, first, *copies, second):
+    for c in (third, fourth, fifth, first, *copies, second):
         c.wait()
     g0 = jnp.broadcast_to(column(gains[0:1, :]), (width, feats))
     g1 = jnp.broadcast_to(column(gains[1:2, :]), (width, feats))
+    count[...] = jnp.full(count.shape, number[0].astype(f32), f32)
+    g2[...] = jnp.broadcast_to(column(gains[2:3, :]), g2.shape)
     bias = jnp.where(live[...] > 0, 0.0, masked_score)
     bias = jnp.concatenate([bias, bias], axis=1)
     last = jnp.where(iota((head, step), 0) == 0, bias, 0.0).astype(bf16)
@@ -219,33 +223,21 @@
     shape = (16 * rows, 16 * rows)
     to, of = iota(shape, 0), iota(shape, 1)
     order = onehot(of == (to % rows) * 16 + to // rows)
-    sent = []
     for b in range(feats // 16):
         x = jnp.concatenate([xn[k * feats + b * 16 : k * feats + b * 16 + 16, :] for k in range(rows)], axis=0)
         moved = nn(order, jnp.concatenate([x, x[:, 128:width]], axis=1))
         out = closed(moved[:, 0:128], moved[:, 128:256])
         at = slice(b * 192, (b + 1) * 192)
-        packed[at, :] = out
-        sent.append(pltpu.make_async_copy(packed.at[at, :], send.at[at, :], out_sems.at[b]))
-        sent[-1].start()
-    for c in sent:
-        c.wait()
-
-
-def prep_kernel(after, qkv, wout, w_in, gain, wt, wo, wi, g2):
-    del after
-    prepare_weights(qkv, wt)
-    wo[...] = wout[...].T
-    wi[...] = w_in[...].T
-    g2[...] = jnp.broadcast_to(column(gain[2:3, :]), g2.shape)
-
-
-def rows_kernel(n_train, got, wt, send, xn, qs, ks, vs, ctx, sbuf):
-    width = wt.shape[-1]
+        send[at, :] = out
+
+
+def rows_kernel(n_train, got, qkv, send, xn, qs, ks, vs, ctx, wt, sbuf):
+    width = qkv.shape[-1]
     head = width // HEADS
     total = xn.shape[0]
+    prepare_weights(qkv, wt)
     fill_constant_rows(qs, vs, head)
-    live = n_train[0]
+    live = jnp.max(n_train[...]).astype(jnp.int32)
     step = 256
 
     def arrived(c):
@@ -327,8 +319,10 @@
         send[b * 192 : (b + 1) * 192, :] = closed(ctx[0:128, at].T.astype(f32), twice.astype(f32))
 
 
-def tail_kernel(got, mid, g2, wo, wi, w_out, result, ctx, out_buf, sems):
+def tail_kernel(got, mid, g2, wout, w_in, w_out, result, ctx, out_buf, sems):
     rows, width, feats = mid.shape
+    wo = wout[...].T
+    wi = w_in[...].T
     shape = (16 * rows, 16 * rows)
     to, of = iota(shape, 0), iota(shape, 1)
     order = onehot(of == (to % 16) * rows + to // 16)
@@ -344,12 +338,12 @@
     for t in range(chunks + 3):
         if t < chunks:
             old = jnp.concatenate([mid[2 * t], mid[2 * t + 1]], axis=1)
-            late[t] = old + nt(wo[...], ctx[t * 2 * feats : (t + 1) * 2 * feats, :])
+            late[t] = old + nt(wo, ctx[t * 2 * feats : (t + 1) * 2 * feats, :])
         if 0 <= t - 2 < chunks:
             v = z.pop(t - 2)
             hidden[t - 2] = (v * 0.5 * (1.0 + lax.erf(v * math.sqrt(0.5)))).astype(bf16)
         if 0 <= t - 1 < chunks:
-            z[t - 1] = nn(wi[...], layer_norm(late[t - 1], g2[...]).astype(bf16))
+            z[t - 1] = nn(wi, layer_norm(late[t - 1], g2[...]).astype(bf16))
         if 0 <= t - 3 < chunks:
             c = t - 3
             out = late.pop(c) + nn(w_out[...], hidden.pop(c))
@@ -362,7 +356,6 @@
 
 
 VMEM = pl.BlockSpec(memory_space=pltpu.VMEM)
-SMEM = pl.BlockSpec(memory_space=pltpu.SMEM)
 ANY = pl.BlockSpec(memory_space=pl.ANY)
 
 
@@ -370,7 +363,7 @@
     return pltpu.with_memory_space_constraint(x, pltpu.VMEM)
 
 
-def front(present, cells, gain, qkv, wout):
+def front(present, cells, gain, qkv, wout, n_train):
     rows, width, feats = cells.shape
     head = width // HEADS
     tokens = rows * feats
@@ -378,55 +371,40 @@
         front_kernel,
         out_shape=(
             pltpu.VMEM(cells.shape, f32),
-            jax.ShapeDtypeStruct((tokens * width // 128, 128), bf16),
+            pltpu.VMEM((tokens * width // 128, 128), bf16),
+            pltpu.VMEM((width, 2 * feats), f32),
+            pltpu.VMEM((8, 128), f32),
         ),
-        in_specs=[ANY] * 5,
-        out_specs=(VMEM, ANY),
+        in_specs=[ANY] * 6,
+        out_specs=(VMEM, VMEM, VMEM, VMEM),
         scratch_shapes=[
             pltpu.VMEM(cells.shape, f32),
             pltpu.VMEM(qkv.shape, bf16),
             pltpu.VMEM(wout.shape, bf16),
             pltpu.VMEM(present.shape, jnp.int32),
             pltpu.VMEM(gain.shape, f32),
-            pltpu.VMEM((tokens * width // 128, 128), bf16),
             pltpu.VMEM((tokens, width), bf16),
             pltpu.VMEM((HEADS // 2, 8 * head, 2 * tokens), bf16),
             pltpu.VMEM((tokens, HEADS * 128), bf16),
             pltpu.VMEM((HEADS * (head + 16), tokens), bf16),
             pltpu.VMEM((width, tokens), bf16),
             pltpu.VMEM((3 * width, width), bf16),
+            pltpu.SMEM((1,), jnp.int32),
             pltpu.SemaphoreType.DMA((rows,)),
-            pltpu.SemaphoreType.DMA((4,)),
-            pltpu.SemaphoreType.DMA((feats // 16,)),
+            pltpu.SemaphoreType.DMA((5,)),
         ],
         name="front",
-    )(present, cells, gain, qkv, wout)
-
-
-def prep(after, qkv, wout, w_in, gain):
-    width, hidden = w_in.shape
-    return pl.pallas_call(
-        prep_kernel,
-        out_shape=(
-            pltpu.VMEM((3 * width, width), bf16),
-            pltpu.VMEM((width, width), bf16),
-            pltpu.VMEM((hidden, width), bf16),
-            pltpu.VMEM((width, 256), f32),
-        ),
-        in_specs=[VMEM] * 5,
-        out_specs=(VMEM, VMEM, VMEM, VMEM),
-        name="prep",
-    )(near(after), qkv, wout, w_in, gain)
-
-
-def rows(n_train, got, wt):
-    width = wt.shape[-1]
+    )(present, cells, gain, qkv, wout, n_train)
+
+
+def rows(n_train, got, qkv):
+    width = qkv.shape[-1]
     head = width // HEADS
     tokens = got.shape[0] * 128 // width
     return pl.pallas_call(
         rows_kernel,
         out_shape=pltpu.VMEM(got.shape, bf16),
-        in_specs=[SMEM, VMEM, VMEM],
+        in_specs=[VMEM, VMEM, VMEM],
         out_specs=VMEM,
         scratch_shapes=[
             pltpu.VMEM((tokens, width), bf16),
@@ -434,13 +412,14 @@
             pltpu.VMEM((tokens, HEADS * 128), bf16),
             pltpu.VMEM((HEADS, head + 16, tokens), bf16),
             pltpu.VMEM((width, tokens), bf16),
+            pltpu.VMEM((3 * width, width), bf16),
             pltpu.VMEM((3, tokens, 256), f32),
         ],
         name="rows",
-    )(n_train, near(got), near(wt))
-
-
-def tail(got, mid, g2, wo, wi, w_out):
+    )(near(n_train), near(got), near(qkv))
+
+
+def tail(got, mid, g2, wout, w_in, w_out):
     rows, width, feats = mid.shape
     return pl.pallas_call(
         tail_kernel,
@@ -453,7 +432,7 @@
             pltpu.SemaphoreType.DMA((rows,)),
         ],
         name="tail",
-    )(near(got), near(mid), near(g2), near(wo), near(wi), near(w_out))
+    )(near(got), near(mid), near(g2), near(wout), near(w_in), near(w_out))
 
 
 def exchanged(block):
@@ -466,12 +445,11 @@
     cells, n_train, present, norm_gain, feat_qkv, feat_out, item_qkv, item_out, mlp_in, mlp_out
 ):
     stood = jnp.transpose(cells, (0, 2, 1))
-    mid, send = front(present.reshape(1, -1), stood, norm_gain, feat_qkv, feat_out)
-    wt, wo, wi, g2 = prep(mid, item_qkv, item_out, mlp_in, norm_gain)
+    mid, send, g2, count = front(present.reshape(1, -1), stood, norm_gain, feat_qkv, feat_out, n_train)
     got = exchanged(send)
-    back = rows(n_train, got, wt)
+    back = rows(count, got, item_qkv)
     returned = exchanged(back)
-    out = tail(returned, mid, g2, wo, wi, jnp.transpose(mlp_out))
+    out = tail(returned, mid, g2, item_out, mlp_in, jnp.transpose(mlp_out))
     return jnp.transpose(out, (0, 2, 1))
 
 

time: 104 us -> 106 us (1.019)
  blocking collectives: 35.2 us -> 91.3 us
  starting transfers between devices: 31 us -> 0 us
  waiting for transfers between devices: 23.1 us -> 0 us
    all_to_all x1 -> x2, blocking collectives: 35.2 us -> 91.3 us  [exchanged(): return lax.all_to_all(tiles, ROW, 0, 0, tiled=True).reshape(block.shape)]
    all_to_all x1 -> x0, starting transfers between devices: 31 us -> none  [exchanged(): return lax.all_to_all(tiles, ROW, 0, 0, tiled=True).reshape(block.shape)]
    all_to_all x1 -> x0, waiting for transfers between devices: 23.1 us -> none  [exchanged(): return lax.all_to_all(tiles, ROW, 0, 0, tiled=True).reshape(block.shape)]
    pallas_call x2 -> x1, Pallas kernels: 6.73 us -> 4.68 us  [front(): pl.pallas_call(front_kernel, out_shape=(pltpu.VMEM(cells.shape, f32), plt...]
    pallas_call x1, Pallas kernels: 3.53 us -> 5.44 us  [rows(): pl.pallas_call(rows_kernel, out_shape=pltpu.VMEM(got.shape, bf16), in_spe...]
  transfers between devices with their start and end apart: 1 -> 0, of which waited for: 1 -> 0; matrix products, arithmetic and copies ran while one was open for 0% -> 0% of each run, Pallas kernels for 1% -> 0%
where the time goes in v8:
time: 106 us; the launch traced here: 105 us
  blocking collectives  91.3 us (86%)
  Pallas kernels  12.6 us (12%)
    all_to_all x2, blocking collectives, exchanged(): return lax.all_to_all(tiles, ROW, 0, 0, tiled=True).reshape(block.shape)  91.3 us
    pallas_call x1, Pallas kernels, rows(): pl.pallas_call(rows_kernel, out_shape=pltpu.VMEM(got.shape, bf16), in_spe...  5.44 us
    pallas_call x1, Pallas kernels, front(): pl.pallas_call(front_kernel, out_shape=(pltpu.VMEM(cells.shape, f32), plt...  4.68 us
    pallas_call x1, Pallas kernels, tail(): pl.pallas_call(tail_kernel, out_shape=jax.ShapeDtypeStruct(mid.shape, f32...  2.48 us

profile of v8, /device:TPU:33, one launch (start us, length us, event | category | flops | bytes accessed | tf_op | source)
XLA Modules:
  0.0 104.8 jit_solution(3021554069309781098)
XLA Ops:
  0.7 4.7 %front.1 = (f32[8,192,128]{2,1,0:T(8,128)S(1)}, bf16[1536,128]{1,0:T(8,128)(2,1)S(1)}, f32[192,256]{1,0:T(8,128)S(1)}, f32[8,128]{1,0:T(8,128)S(1)}) custom-call(s32[1,128]{1,0:T(1,128)} %bitcast.14, f32[8,192,128]{2,1,0:T(8,128)} %bitcast.13, f32[3,192]{1,0:T(4,128)} %gain.1, bf16[3,192,192]{2,1,0:T(8,128)(2,1)} %qkv.2, bf16[192,192]{1,0:T(8,128)(2,1)} %wout.2, ...), custom_call_target="tpu_custom_call" | custom-call | tf_op jit(solution)/shard_map/front/pallas_call | solution.py:370
  5.3 0.0 copy-start
  5.4 56.1 %all_to_all.10 = bf16[128,3,4,128]{3,2,1,0:T(4,128)(2,1)S(1)} all-to-all(bf16[128,3,4,128]{3,2,1,0:T(4,128)(2,1)S(1)} %bitcast.11), channel_id=1, replica_groups=mesh['grp'=2,'row'=128] {'row'}, dimensions={0} | all-to-all | bytes 786432 | tf_op jit(solution)/shard_map/all_to_all | solution.py:441
  61.5 0.0 copy-done
  61.5 5.4 %rows.1 = bf16[1536,128]{1,0:T(8,128)(2,1)S(1)} custom-call(f32[8,128]{1,0:T(8,128)S(1)} %get-tuple-element.9.n_train, bf16[1536,128]{1,0:T(8,128)(2,1)S(1)} %bitcast.8, bf16[3,192,192]{2,1,0:T(8,128)(2,1)S(1)} %copy-done), custom_call_target="tpu_custom_call" | custom-call | tf_op jit(solution)/shard_map/rows/pallas_call | solution.py:404
  66.9 0.0 copy-start.1
  66.9 0.0 copy-start.2
  66.9 0.0 copy-start.3
  66.9 35.2 %all_to_all.11 = bf16[128,3,4,128]{3,2,1,0:T(4,128)(2,1)S(1)} all-to-all(bf16[128,3,4,128]{3,2,1,0:T(4,128)(2,1)S(1)} %bitcast.9), channel_id=1, replica_groups=mesh['grp'=2,'row'=128] {'row'}, dimensions={0} | all-to-all | bytes 786432 | tf_op jit(solution)/shard_map/all_to_all | solution.py:441
  102.1 0.0 copy-done.1
  102.1 0.0 copy-done.2
  102.1 0.0 copy-done.3
  102.1 2.5 %tail.1 = f32[8,192,128]{2,1,0:T(8,128)} custom-call(bf16[1536,128]{1,0:T(8,128)(2,1)S(1)} %bitcast.10, f32[8,192,128]{2,1,0:T(8,128)S(1)} %get-tuple-element.11.mid, f32[192,256]{1,0:T(8,128)S(1)} %get-tuple-element.12.g2, bf16[192,192]{1,0:T(8,128)(2,1)S(1)} %copy-done.3, bf16[192,768]{1,0:T(8,128)(2,1)S(1)} %copy-done.1, bf16[192,768]{1,0:T(8,128)(2,1)S(1)} %bitcast.12), custom_call_target="tpu_custom_call" | custom-call | tf_op jit(solution)/shard_map/tail/pallas_call | solution.py:424
Async XLA Ops:
  5.3 56.1 %copy-start = (bf16[3,192,192]{2,1,0:T(8,128)(2,1)S(1)}, bf16[3,192,192]{2,1,0:T(8,128)(2,1)}, u32[]{:S(2)}) copy-start(bf16[3,192,192]{2,1,0:T(8,128)(2,1)} %qkv.3) | copy-start | bytes 663556
  66.9 35.2 %copy-start.1 = (bf16[192,768]{1,0:T(8,128)(2,1)S(1)}, bf16[192,768]{1,0:T(8,128)(2,1)}, u32[]{:S(2)}) copy-start(bf16[192,768]{1,0:T(8,128)(2,1)} %w_in.1) | copy-start | bytes 884740
  66.9 35.2 %copy-start.2 = (bf16[768,192]{0,1:T(8,128)(2,1)S(1)}, bf16[768,192]{0,1:T(8,128)(2,1)}, u32[]{:S(2)}) copy-start(bf16[768,192]{0,1:T(8,128)(2,1)} %param.19) | copy-start | bytes 884740
  66.9 35.2 %copy-start.3 = (bf16[192,192]{1,0:T(8,128)(2,1)S(1)}, bf16[192,192]{1,0:T(8,128)(2,1)}, u32[]{:S(2)}) copy-start(bf16[192,192]{1,0:T(8,128)(2,1)} %wout.3) | copy-start | bytes 221188
